TPU v7x, 16 devices: a whole 2x2x2 slice. The times are simulated.
16 devices in a mesh: dp: 4 (over z, y), sp: 4 (over x, core).
Axes of the slice: x: 2, y: 2, z: 2, core: 2. Of those that a mesh axis runs over, the one named last changes fastest.
Arguments:
- x_steps: bfloat16 [4, 256, 4096], P(None, 'dp'), parts along dimension 1
- k_cache: bfloat16 [256, 512, 8, 128], P('dp', 'sp'), parts along dimension 0
- v_cache: bfloat16 [256, 512, 8, 128], P('dp', 'sp'), parts along dimension 0
- seq_lens: int32 [256], P('dp'), parts along dimension 0
- norm_gain: bfloat16 [4096], replicated
- w_q: bfloat16 [4096, 4096], replicated
- w_k: bfloat16 [4096, 1024], replicated
- w_v: bfloat16 [4096, 1024], replicated
- w_o: bfloat16 [4096, 4096], replicated
- q_gain: bfloat16 [128], replicated
- k_gain: bfloat16 [128], replicated
Outputs:
- output 1: bfloat16 [4, 256, 4096], P(None, 'dp'), parts along dimension 1
- output 2: bfloat16 [256, 512, 8, 128], P('dp', 'sp'), parts along dimension 0
- output 3: bfloat16 [256, 512, 8, 128], P('dp', 'sp'), parts along dimension 0
There are 4 independent parts. A program takes and returns all parts, laid end to end along the dimension named above; an argument that names none is the same for every part.
All inputs are finite; a program needn't handle non-finite values.
Results may differ from a plain program's by a relative error of at most 0.0105101.
Values sent between devices are 32-bit elements.
A program may use at most 1 GiB of HBM per device.

v0:
```python
import functools
import math

import jax
import jax.numpy as jnp
from jax import lax
from jax.experimental import pallas as pl
from jax.experimental.pallas import tpu as pltpu
from jax.sharding import PartitionSpec as P

NORM_EPS = 1e-6
ROPE_BASE = 1000000.0
MASKED_MAX = -1e30
HEAD_DIM = 128
F32 = jnp.float32
BF16 = jnp.bfloat16
MIB = 1024 * 1024
VMEM = pltpu.VMEM
DMA = pltpu.SemaphoreType.DMA
IN_VMEM = pl.BlockSpec(memory_space=VMEM)
IN_PLACE = pl.BlockSpec(memory_space=pl.ANY)


def small_tables(seq_lens, steps, norm_gain, q_gain, k_gain):
    half = HEAD_DIM // 2
    positions = (seq_lens[None, :] + jnp.arange(steps, dtype=jnp.int32)[:, None]).reshape(-1)
    inv_freq = jnp.exp(jnp.arange(half, dtype=F32) * (-2.0 * math.log(ROPE_BASE) / HEAD_DIM))
    angles = positions.astype(F32)[:, None] * inv_freq
    cosine = jnp.cos(angles)
    sine = jnp.sin(angles)
    rope = jnp.concatenate([jnp.concatenate([cosine, cosine], axis=-1), jnp.concatenate([-sine, sine], axis=-1)], axis=0)
    gains = jnp.concatenate([norm_gain, q_gain, k_gain]).astype(F32).reshape(-1, HEAD_DIM)
    return rope, gains


def remote(src, dst, sems, peer):
    return pltpu.make_async_remote_copy(src_ref=src, dst_ref=dst, send_sem=sems.at[0], recv_sem=sems.at[1], device_id={'sp': peer}, device_id_type=pl.DeviceIdType.MESH)


def meet(*peers):
    barrier = pltpu.get_barrier_semaphore()
    for peer in peers:
        pl.semaphore_signal(barrier, inc=1, device_id={'sp': peer}, device_id_type=pl.DeviceIdType.MESH)
    pl.semaphore_wait(barrier, len(peers))


def project_kernel(width, heads, kv_heads, x_hbm, rope_ref, gain_ref, wq_hbm, wk_hbm, wv_hbm, q_ref, k_ref, v_ref, x_rows, normed, acc, wbuf, sem_x, sems_w, sems_q, sems_k, sems_v):
    rows, hidden = x_rows.shape
    per_block = width // HEAD_DIM
    core = lax.rem(lax.axis_index('sp'), 2)
    other_core = lax.axis_index('sp') + 1 - 2 * core

    x_copy = pltpu.make_async_copy(x_hbm, x_rows, sem_x)
    x_copy.start()
    blocks = [(wk_hbm, k_ref, sems_k, kv_heads, 0)]
    blocks += [(wq_hbm, q_ref, sems_q, heads, i) for i in range(heads // 2 // per_block)]
    blocks += [(wv_hbm, v_ref, sems_v, kv_heads, 0)]
    w_copies = []
    for n, (w_hbm, _, _, total, i) in enumerate(blocks):
        cols = pl.ds(pl.multiple_of(core * (total // 2 * HEAD_DIM) + i * width, width), width)
        copy = pltpu.make_async_copy(w_hbm.at[:, cols], wbuf.at[n], sems_w.at[n])
        copy.start()
        w_copies.append(copy)

    meet(other_core)
    x_copy.wait()

    @pl.loop(0, rows // 16)
    def _(i):
        here = pl.ds(pl.multiple_of(i * 16, 16), 16)
        values = x_rows[here, :].astype(F32)
        inv_rms = lax.rsqrt(jnp.mean(values * values, axis=-1, keepdims=True) + NORM_EPS)
        for n in range(hidden // HEAD_DIM):
            lanes = slice(n * HEAD_DIM, (n + 1) * HEAD_DIM)
            normed[here, lanes] = (x_rows[here, lanes].astype(F32) * inv_rms * gain_ref[n:n + 1, :]).astype(BF16)

    def finish(n):
        w_hbm, out_ref, sems, total, i = blocks[n]
        first = core * (total // 2) + i * per_block
        for j in range(per_block):
            values = acc[n % 2, :, j * HEAD_DIM:(j + 1) * HEAD_DIM].astype(BF16).astype(F32)
            if out_ref is not v_ref:
                row = hidden // HEAD_DIM + (1 if out_ref is k_ref else 0)
                inv_rms = lax.rsqrt(jnp.mean(values * values, axis=-1, keepdims=True) + NORM_EPS)
                scaled = values * inv_rms * gain_ref[row:row + 1, :]
                values = scaled * rope_ref[:rows, :] + pltpu.roll(scaled, HEAD_DIM // 2, 1) * rope_ref[rows:, :]
                values = values.astype(BF16).astype(F32)
            out_ref[:, first + j, :, :] = values.reshape(rows // 8, 8, HEAD_DIM)

    def send(n):
        _, out_ref, sems, total, i = blocks[n]
        there = pl.ds(core * (total // 2) + i * per_block, per_block)
        copy = remote(out_ref.at[:, there], out_ref.at[:, there], sems.at[i], other_core)
        copy.start()
        return copy

    sends = []
    for n in range(len(blocks)):
        w_copies[n].wait()
        acc[n % 2] = jnp.dot(normed[...], wbuf[n], preferred_element_type=F32)
        if n > 0:
            finish(n - 1)
            sends.append(send(n - 1))
    finish(len(blocks) - 1)
    sends.append(send(len(blocks) - 1))
    for copy in sends:
        copy.wait()


def project(x_steps, rope, gains, w_q, w_k, w_v):
    steps, batch, hidden = x_steps.shape
    rows = steps * batch
    heads = w_q.shape[1] // HEAD_DIM
    kv_heads = w_k.shape[1] // HEAD_DIM
    width = kv_heads // 2 * HEAD_DIM
    q_blocks = heads // kv_heads
    return pl.pallas_call(
        functools.partial(project_kernel, width, heads, kv_heads),
        name='project',
        out_shape=tuple(jax.ShapeDtypeStruct((rows // 8, n, 8, HEAD_DIM), F32) for n in (heads, kv_heads, kv_heads)),
        in_specs=[IN_PLACE, IN_VMEM, IN_VMEM] + [IN_PLACE] * 3,
        out_specs=(IN_VMEM,) * 3,
        scratch_shapes=[
            VMEM((rows, hidden), BF16),
            VMEM((rows, hidden), BF16),
            VMEM((2, rows, width), F32),
            VMEM((q_blocks + 2, hidden, width), BF16),
            DMA,
            DMA((q_blocks + 2,)),
            DMA((q_blocks, 2)),
            DMA((1, 2)),
            DMA((1, 2)),
        ],
        compiler_params=pltpu.CompilerParams(collective_id=1, has_side_effects=True, vmem_limit_bytes=40 * MIB),
    )(x_steps.reshape(rows, hidden), rope, gains, w_q, w_k, w_v)


def attend_kernel(steps, group, depth, lens_ref, k_hbm, v_hbm, q_ref, kn_ref, vn_ref, ko_hbm, vo_hbm, num_ref, stat_ref, k_buf, v_buf, dist, sems_in, sems_out):
    slots_held, _, key_rows, _ = k_buf.shape
    batch = lens_ref.shape[0]
    heads, kv_heads = q_ref.shape[0] // (steps * batch), kn_ref.shape[0] // (steps * batch)
    slots = key_rows // kv_heads
    rows = steps * heads
    half = heads // 2
    first_slot = lax.axis_index('sp') * slots
    lane = lax.broadcasted_iota(jnp.int32, (rows, 128), 1)
    upper = lax.broadcasted_iota(jnp.int32, (2 * kv_heads, HEAD_DIM), 0) >= kv_heads
    scale = HEAD_DIM ** -0.5 * math.log2(math.e)
    groups = batch // group

    def copies_in(g, slot):
        here = pl.ds(g * group, group)
        return (pltpu.make_async_copy(k_hbm.at[here], k_buf.at[slot], sems_in.at[slot, 0]),
                pltpu.make_async_copy(v_hbm.at[here], v_buf.at[slot], sems_in.at[slot, 1]))

    def copies_out(g, slot):
        here = pl.ds(g * group, group)
        return (pltpu.make_async_copy(k_buf.at[slot], ko_hbm.at[here], sems_out.at[slot, 0]),
                pltpu.make_async_copy(v_buf.at[slot], vo_hbm.at[here], sems_out.at[slot, 1]))

    for g in range(depth):
        for copy in copies_in(g, g):
            copy.start()

    stat_ref[...] = jnp.where(lane < batch, MASKED_MAX, 0.0)
    row = lax.broadcasted_iota(jnp.int32, (rows, key_rows), 0)
    col = lax.broadcasted_iota(jnp.int32, (rows, key_rows), 1)
    row_half, in_half = row // (steps * half), lax.rem(row, steps * half)
    row_kv = (row_half * half + lax.rem(in_half, half)) // (heads // kv_heads)
    dist[...] = jnp.where(row_kv == lax.rem(col, kv_heads), col // kv_heads - in_half // half, 1 << 24)

    def one_group(g, carry):
        slot = lax.rem(g, slots_held)
        for copy in copies_in(g, slot):
            copy.wait()

        for s in range(group):
            b = g * group + s
            rel = lens_ref[b] - first_slot
            for t in range(steps):
                at = rel + t

                @pl.when((at >= 0) & (at < slots))
                def _():
                    base = pl.multiple_of((at >> 1) * (2 * kv_heads), 2 * kv_heads)
                    mine = upper == ((at & 1) == 1)
                    r = t * batch + b
                    new_rows = pl.ds((r >> 3) * (8 * kv_heads) + (r & 7), kv_heads, stride=8)
                    for buf, new in ((k_buf, kn_ref), (v_buf, vn_ref)):
                        fresh = new[new_rows, :]
                        fresh = jnp.concatenate([fresh, fresh], axis=0)
                        old = buf[slot, s, pl.ds(base, 2 * kv_heads), :].astype(F32)
                        buf[slot, s, pl.ds(base, 2 * kv_heads), :] = jnp.where(mine, fresh, old).astype(BF16)

        rels = [lens_ref[g * group + s] - first_slot for s in range(group)]
        longest = functools.reduce(jnp.maximum, rels)
        visible = longest + steps - 1 >= 0

        @pl.when(visible)
        def _():
            stats = stat_ref[...]
            for s in range(group):
                b = g * group + s
                pieces = []
                for h in range(2):
                    for t in range(steps):
                        r = t * batch + b
                        start = (r >> 3) * (8 * heads) + (r & 7) + h * (8 * half)
                        pieces.append(q_ref[pl.ds(start, half, stride=8), :].astype(BF16))
                query = jnp.concatenate(pieces, axis=0)
                scores = lax.dot_general(query, k_buf[slot, s], (((1,), (1,)), ((), ())), preferred_element_type=F32)
                scores = jnp.where(dist[...] <= rels[s], scores, -jnp.inf)
                row_max = jnp.maximum(jnp.max(scores, axis=1, keepdims=True), MASKED_MAX)
                weights = jnp.exp2((scores - row_max) * scale)
                row_sum = jnp.sum(weights, axis=1, keepdims=True)
                num_ref[b] = jnp.dot(weights.astype(BF16), v_buf[slot, s], preferred_element_type=F32)
                stats = jnp.where(lane == b, row_max, stats)
                stats = jnp.where(lane == b + batch, row_sum, stats)
            stat_ref[...] = stats

        @pl.when(jnp.logical_not(visible))
        def _():
            for s in range(group):
                num_ref[g * group + s] = jnp.zeros((rows, HEAD_DIM), F32)

        for copy in copies_out(g, slot):
            copy.start()
        ahead = g + depth
        next_slot = lax.rem(ahead, slots_held)

        @pl.when(ahead < groups)
        def _():
            @pl.when(ahead >= slots_held)
            def _():
                for copy in copies_out(ahead - slots_held, next_slot):
                    copy.wait()

            for copy in copies_in(ahead, next_slot):
                copy.start()

        return carry

    lax.fori_loop(0, groups, one_group, 0)
    for g in range(groups - slots_held, groups):
        for copy in copies_out(g, g % slots_held):
            copy.wait()


def attend(seq_lens, k_cache, v_cache, queries, k_new, v_new, steps):
    batch, slots, kv_heads, head_dim = k_cache.shape
    heads = queries.shape[1]
    rows = steps * heads
    key_rows = slots * kv_heads
    group, depth, held = 2, 5, 8
    cache = jax.ShapeDtypeStruct((batch, key_rows, head_dim), BF16)
    k_out, v_out, numer, stats = pl.pallas_call(
        functools.partial(attend_kernel, steps, group, depth),
        name='attend',
        in_specs=[pl.BlockSpec(memory_space=pltpu.SMEM), IN_PLACE, IN_PLACE, IN_VMEM, IN_VMEM, IN_VMEM],
        out_specs=(IN_PLACE, IN_PLACE, IN_VMEM, IN_VMEM),
        out_shape=(cache, cache, jax.ShapeDtypeStruct((batch, rows, head_dim), F32), jax.ShapeDtypeStruct((rows, 128), F32)),
        scratch_shapes=[
            VMEM((held, group, key_rows, head_dim), BF16),
            VMEM((held, group, key_rows, head_dim), BF16),
            VMEM((rows, key_rows), jnp.int32),
            DMA((held, 2)),
            DMA((held, 2)),
        ],
        compiler_params=pltpu.CompilerParams(vmem_limit_bytes=32 * MIB),
    )(seq_lens, k_cache.reshape(batch, key_rows, head_dim), v_cache.reshape(batch, key_rows, head_dim), queries.reshape(-1, head_dim), k_new.reshape(-1, head_dim), v_new.reshape(-1, head_dim))
    return k_out.reshape(k_cache.shape), v_out.reshape(v_cache.shape), numer, stats


def merge_kernel(chunks, steps, numer, stats, wo_hbm, y_own, y_other, wo, stat_d, stat_send, stat_x, recv_d, send_x, recv_x, scaled, att_f32, attended, sems_w, sem_stat, sems_d, sems_x, sems_y):
    _, batch, hidden = y_own.shape
    rows = numer.shape[1] // 2
    half = rows // steps
    me = lax.axis_index('sp')
    core = lax.rem(me, 2)
    other_core = me + 1 - 2 * core
    other_chip = lax.rem(me + 2, 4)
    own = pl.ds(pl.multiple_of(core * rows, rows), rows)
    other = pl.ds(pl.multiple_of((1 - core) * rows, rows), rows)
    firsts = [sum(chunks[:c]) for c in range(len(chunks))]

    w_pieces = sems_w.shape[0]
    w_rows = half * HEAD_DIM // w_pieces
    w_first = core * (half * HEAD_DIM)
    meet(other_core, other_chip)

    stat_copy = remote(stats.at[other], stat_d, sem_stat.at[0], other_core)
    stat_copy.start()
    core_copies = []
    for c, (first, seqs) in enumerate(zip(firsts, chunks)):
        here = pl.ds(first, seqs)
        copy = remote(numer.at[here, other], recv_d.at[here], sems_d.at[c], other_core)
        copy.start()
        core_copies.append(copy)
    w_copies = []
    for p in range(w_pieces):
        src = wo_hbm.at[pl.ds(pl.multiple_of(w_first + p * w_rows, w_rows), w_rows), :]
        copy = pltpu.make_async_copy(src, wo.at[pl.ds(p * w_rows, w_rows), :], sems_w.at[p])
        copy.start()
        w_copies.append(copy)

    lane = lax.broadcasted_iota(jnp.int32, (rows, 128), 1)
    scale = HEAD_DIM ** -0.5

    def combine(mine, theirs):
        top = jnp.maximum(mine, theirs)
        fac_a, fac_b = jnp.exp((mine - top) * scale), jnp.exp((theirs - top) * scale)
        total = pltpu.roll(mine, 128 - batch, 1) * fac_a + pltpu.roll(theirs, 128 - batch, 1) * fac_b
        return top, fac_a, fac_b, total

    stat_copy.wait()
    top, fac_a, fac_b, total = combine(stats[own, :], stat_d[...])
    stat_send[...] = jnp.where(lane < batch, top, pltpu.roll(total, batch, 1))
    scaled[0] = fac_a
    scaled[1] = fac_b
    chip_stat_copy = remote(stat_send, stat_x, sem_stat.at[1], other_chip)
    chip_stat_copy.start()

    chip_copies = []
    for c, (first, seqs) in enumerate(zip(firsts, chunks)):
        core_copies[c].wait()
        for b in range(first, first + seqs):
            send_x[b] = numer[b, own, :] * scaled[0, :, b:b + 1] + recv_d[b] * scaled[1, :, b:b + 1]
        here = pl.ds(first, seqs)
        copy = remote(send_x.at[here], recv_x.at[here], sems_x.at[c], other_chip)
        copy.start()
        chip_copies.append(copy)

    chip_stat_copy.wait()
    _, fac_a, fac_b, total = combine(stat_send[...], stat_x[...])
    scaled[0] = fac_a / total
    scaled[1] = fac_b / total

    width = 512
    y_copies = []
    for c, (first, seqs) in enumerate(zip(firsts, chunks)):
        chip_copies[c].wait()
        for b in range(first, first + seqs):
            merged = send_x[b] * scaled[0, :, b:b + 1] + recv_x[b] * scaled[1, :, b:b + 1]
            att_f32[pl.ds((b - first) * rows, rows), :] = merged
        for t in range(steps):
            for h in range(half):
                values = att_f32[pl.ds(t * half + h, seqs, stride=rows), :]
                attended[t * seqs:(t + 1) * seqs, h * HEAD_DIM:(h + 1) * HEAD_DIM] = values
        if c == 0:
            for copy in w_copies:
                copy.wait()

        @pl.loop(0, hidden // width)
        def _(j):
            cols = pl.ds(pl.multiple_of(j * width, width), width)
            out = jnp.dot(attended[:steps * seqs, :].astype(BF16), wo[:, cols], preferred_element_type=F32)
            for t in range(steps):
                y_own[t, first:first + seqs, cols] = out[t * seqs:(t + 1) * seqs, :]

        here = pl.ds(first, seqs)
        copy = remote(y_own.at[:, here, :], y_other.at[:, here, :], sems_y.at[c], other_core)
        copy.start()
        y_copies.append(copy)
    for copy in y_copies:
        copy.wait()


def merge(numer, stats, w_o, steps):
    batch, rows, _ = numer.shape
    hidden = w_o.shape[1]
    chunks = (16, 16, 16, 8, 8)
    largest = max(chunks)
    part = jax.ShapeDtypeStruct((steps, batch, hidden), F32)
    stat = VMEM((rows // 2, 128), F32)
    return pl.pallas_call(
        functools.partial(merge_kernel, chunks, steps),
        name='merge',
        out_shape=(part, part),
        in_specs=[IN_VMEM, IN_VMEM, IN_PLACE],
        out_specs=(IN_VMEM, IN_VMEM),
        scratch_shapes=[
            VMEM((w_o.shape[0] // 2, hidden), BF16),
            stat,
            stat,
            stat,
            VMEM((batch, rows // 2, HEAD_DIM), F32),
            VMEM((batch, rows // 2, HEAD_DIM), F32),
            VMEM((batch, rows // 2, HEAD_DIM), F32),
            VMEM((2, rows // 2, 128), F32),
            VMEM((largest * rows // 2, HEAD_DIM), F32),
            VMEM((steps * largest, w_o.shape[0] // 2), F32),
            DMA((8,)),
            DMA((2, 2)),
            DMA((len(chunks), 2)),
            DMA((len(chunks), 2)),
            DMA((len(chunks), 2)),
        ],
        compiler_params=pltpu.CompilerParams(collective_id=0, has_side_effects=True, vmem_limit_bytes=40 * MIB),
    )(numer, stats, w_o)


def solution(mesh):
    def per_device(x_steps, k_local, v_local, seq_lens, norm_gain, w_q, w_k, w_v, w_o, q_gain, k_gain):
        steps = x_steps.shape[0]
        rope, gains = small_tables(seq_lens, steps, norm_gain, q_gain, k_gain)
        queries, keys_new, vals_new = project(x_steps, rope, gains, w_q, w_k, w_v)
        k_out, v_out, numer, stats = attend(seq_lens, k_local, v_local, queries, keys_new, vals_new, steps)
        own, other = merge(numer, stats, w_o, steps)
        y_steps = (x_steps.astype(F32) + (own + other)).astype(BF16)
        return y_steps, k_out, v_out

    cache_spec = P('dp', 'sp', None, None)
    step_spec = P(None, 'dp', None)
    return jax.shard_map(per_device, mesh=mesh, in_specs=(step_spec, cache_spec, cache_spec, P('dp'), P(), P(), P(), P(), P(), P(), P()), out_specs=(step_spec, cache_spec, cache_spec), check_vma=False)
```

profile of v0, /device:TPU:0, one launch (start us, length us, event | category | flops | bytes accessed | tf_op | source)
XLA Modules:
  0.0 111.0 jit_solution(7049161981179397268)
XLA Ops:
  0.6 0.7 add_convert_fusion.1
  1.3 0.1 convert_element_type.25
  1.4 0.7 fusion.1.gain_ref
  2.1 0.5 multiply_cosine_fusion
  2.7 0.1 maximum_maximum_fusion.rope_ref
  2.8 0.0 copy-start
  2.8 1.6 %copy-done = bf16[4,64,4096]{2,1,0:T(8,128)(2,1)S(1)} copy-done((bf16[4,64,4096]{2,1,0:T(8,128)(2,1)S(1)}, bf16[4,64,4096]{2,1,0:T(8,128)(2,1)}, u32[]{:S(2)}) %copy-start) | copy-done | bytes 2097176
  4.4 0.0 copy-start.2
  4.4 13.1 %project.1 = (f32[32,32,8,128]{3,2,1,0:T(8,128)S(1)}, f32[32,8,8,128]{3,2,1,0:T(8,128)S(1)}, f32[32,8,8,128]{3,2,1,0:T(8,128)S(1)}) custom-call(bf16[256,4096]{1,0:T(8,128)(2,1)S(1)} %bitcast.13, f32[512,128]{1,0:T(8,128)S(1)} %maximum_maximum_fusion.rope_ref, f32[34,128]{1,0:T(8,128)S(1)} %fusion.1.gain_ref, bf16[4096,4096]{1,0:T(8,128)(2,1)} %wq_hbm.1, ...), custom_call_target="tpu_custom_call" | custom-call | tf_op jit(solution)/shard_map/project/pallas_call | solution.py:117
  17.5 0.0 copy-done.2
  17.5 35.0 %attend.1 = (bf16[64,1024,128]{2,1,0:T(8,128)(2,1)}, bf16[64,1024,128]{2,1,0:T(8,128)(2,1)}, f32[64,128,128]{2,1,0:T(8,128)S(1)}, f32[128,128]{1,0:T(8,128)S(1)}) custom-call(s32[64]{0:T(128)S(1)} %copy-done.2, bf16[64,1024,128]{2,1,0:T(8,128)(2,1)} %bitcast.17, bf16[64,1024,128]{2,1,0:T(8,128)(2,1)} %bitcast.18, f32[8192,128]{1,0:T(8,128)S(1)} %bitcast.14, ...), custom_call_target="tpu_custom_call" | custom-call | tf_op jit(solution)/shard_map/attend/pallas_call | solution.py:256
  52.5 0.0 copy-start.1
  52.5 56.2 %merge.1 = (f32[4,64,4096]{2,1,0:T(8,128)S(1)}, f32[4,64,4096]{2,1,0:T(8,128)S(1)}) custom-call(f32[64,128,128]{2,1,0:T(8,128)S(1)} %get-tuple-element.15.numer, f32[128,128]{1,0:T(8,128)S(1)} %get-tuple-element.16.stats, bf16[4096,4096]{1,0:T(8,128)(2,1)} %wo_hbm.1), custom_call_target="tpu_custom_call" | custom-call | tf_op jit(solution)/shard_map/merge/pallas_call | solution.py:375
  108.7 0.0 copy-done.1
  108.7 2.3 %add_convert_fusion = bf16[4,64,4096]{2,1,0:T(8,128)(2,1)} fusion(f32[4,64,4096]{2,1,0:T(8,128)S(1)} %get-tuple-element.17, f32[4,64,4096]{2,1,0:T(8,128)S(1)} %get-tuple-element.18, bf16[4,64,4096]{2,1,0:T(8,128)(2,1)S(1)} %copy-done.1), kind=kLoop, calls=%fused_computation | loop fusion | flops 4194304 | bytes 12582912 | tf_op jit(solution)/shard_map/convert_element_type | solution.py:409
  (1 shorter events, 0.0 us)
Async XLA Ops:
  2.8 1.6 %copy-start = (bf16[4,64,4096]{2,1,0:T(8,128)(2,1)S(1)}, bf16[4,64,4096]{2,1,0:T(8,128)(2,1)}, u32[]{:S(2)}) copy-start(bf16[4,64,4096]{2,1,0:T(8,128)(2,1)} %param.11) | copy-start | bytes 6291460
  4.4 13.1 %copy-start.2 = (s32[64]{0:T(128)S(1)}, s32[64]{0:T(128)}, u32[]{:S(2)}) copy-start(s32[64]{0:T(128)} %lens_ref.1) | copy-start | bytes 772
  52.5 56.2 %copy-start.1 = (bf16[4,64,4096]{2,1,0:T(8,128)(2,1)S(1)}, bf16[4,64,4096]{2,1,0:T(8,128)(2,1)}, u32[]{:S(2)}) copy-start(bf16[4,64,4096]{2,1,0:T(8,128)(2,1)} %param.11) | copy-start | bytes 6291460
where the time goes:
time: 111 us
  Pallas kernels  104 us (94%)
  other arithmetic  4.36 us (4%)
  local copies, waits for them, and re-layouts  1.68 us (2%)
    pallas_call x1, Pallas kernels, merge(): pl.pallas_call(functools.partial(merge_kernel, chunks, steps), name='merg...  56.2 us
    pallas_call x1, Pallas kernels, attend(): pl.pallas_call(functools.partial(attend_kernel, steps, group, depth), nam...  35 us
    pallas_call x1, Pallas kernels, project(): pl.pallas_call(functools.partial(project_kernel, width, heads, kv_heads),...  13.1 us
    convert_element_type x1, other arithmetic, per_device(): y_steps = (x_steps.astype(F32) + (own + other)).astype(BF16)  2.28 us

commit v1 on v0

--- a/solution.py
+++ b/solution.py
@@ -118,7 +118,7 @@
         functools.partial(project_kernel, width, heads, kv_heads),
         name='project',
         out_shape=tuple(jax.ShapeDtypeStruct((rows // 8, n, 8, HEAD_DIM), F32) for n in (heads, kv_heads, kv_heads)),
-        in_specs=[IN_PLACE, IN_VMEM, IN_VMEM] + [IN_PLACE] * 3,
+        in_specs=[pl.BlockSpec(memory_space=pltpu.HBM), IN_VMEM, IN_VMEM] + [IN_PLACE] * 3,
         out_specs=(IN_VMEM,) * 3,
         scratch_shapes=[
             VMEM((rows, hidden), BF16),
@@ -135,33 +135,33 @@
     )(x_steps.reshape(rows, hidden), rope, gains, w_q, w_k, w_v)
 
 
-def attend_kernel(steps, group, depth, lens_ref, k_hbm, v_hbm, q_ref, kn_ref, vn_ref, ko_hbm, vo_hbm, num_ref, stat_ref, k_buf, v_buf, dist, sems_in, sems_out):
-    slots_held, _, key_rows, _ = k_buf.shape
+def attend_kernel(steps, depth, lens_ref, k_hbm, v_hbm, q_ref, kn_ref, vn_ref, ko_hbm, vo_hbm, num_ref, stat_ref, k_buf, v_buf, dist, scores_0, scores_1, weights_0, weights_1, sems_in, sems_out):
+    held, key_rows, _ = k_buf.shape
     batch = lens_ref.shape[0]
     heads, kv_heads = q_ref.shape[0] // (steps * batch), kn_ref.shape[0] // (steps * batch)
     slots = key_rows // kv_heads
     rows = steps * heads
     half = heads // 2
     first_slot = lax.axis_index('sp') * slots
-    lane = lax.broadcasted_iota(jnp.int32, (rows, 128), 1)
     upper = lax.broadcasted_iota(jnp.int32, (2 * kv_heads, HEAD_DIM), 0) >= kv_heads
     scale = HEAD_DIM ** -0.5 * math.log2(math.e)
-    groups = batch // group
-
-    def copies_in(g, slot):
-        here = pl.ds(g * group, group)
-        return (pltpu.make_async_copy(k_hbm.at[here], k_buf.at[slot], sems_in.at[slot, 0]),
-                pltpu.make_async_copy(v_hbm.at[here], v_buf.at[slot], sems_in.at[slot, 1]))
-
-    def copies_out(g, slot):
-        here = pl.ds(g * group, group)
-        return (pltpu.make_async_copy(k_buf.at[slot], ko_hbm.at[here], sems_out.at[slot, 0]),
-                pltpu.make_async_copy(v_buf.at[slot], vo_hbm.at[here], sems_out.at[slot, 1]))
-
-    for g in range(depth):
-        for copy in copies_in(g, g):
+    scores_refs, weights_refs = (scores_0, scores_1), (weights_0, weights_1)
+
+    def copies_in(b):
+        slot = lax.rem(b, held)
+        return (pltpu.make_async_copy(k_hbm.at[b], k_buf.at[slot], sems_in.at[slot, 0]),
+                pltpu.make_async_copy(v_hbm.at[b], v_buf.at[slot], sems_in.at[slot, 1]))
+
+    def copies_out(b):
+        slot = lax.rem(b, held)
+        return (pltpu.make_async_copy(k_buf.at[slot], ko_hbm.at[b], sems_out.at[slot, 0]),
+                pltpu.make_async_copy(v_buf.at[slot], vo_hbm.at[b], sems_out.at[slot, 1]))
+
+    for b in range(depth):
+        for copy in copies_in(b):
             copy.start()
 
+    lane = lax.broadcasted_iota(jnp.int32, (rows, 128), 1)
     stat_ref[...] = jnp.where(lane < batch, MASKED_MAX, 0.0)
     row = lax.broadcasted_iota(jnp.int32, (rows, key_rows), 0)
     col = lax.broadcasted_iota(jnp.int32, (rows, key_rows), 1)
@@ -169,80 +169,109 @@
     row_kv = (row_half * half + lax.rem(in_half, half)) // (heads // kv_heads)
     dist[...] = jnp.where(row_kv == lax.rem(col, kv_heads), col // kv_heads - in_half // half, 1 << 24)
 
-    def one_group(g, carry):
-        slot = lax.rem(g, slots_held)
-        for copy in copies_in(g, slot):
+    def rel_of(b):
+        return lens_ref[jnp.clip(b, 0, batch - 1)] - first_slot
+
+    def receive(b):
+        slot = lax.rem(b, held)
+        for copy in copies_in(b):
             copy.wait()
-
-        for s in range(group):
-            b = g * group + s
-            rel = lens_ref[b] - first_slot
+        rel = rel_of(b)
+        for t in range(steps):
+            at = rel + t
+
+            @pl.when((at >= 0) & (at < slots))
+            def _():
+                base = pl.multiple_of((at >> 1) * (2 * kv_heads), 2 * kv_heads)
+                mine = upper == ((at & 1) == 1)
+                r = t * batch + b
+                new_rows = pl.ds((r >> 3) * (8 * kv_heads) + (r & 7), kv_heads, stride=8)
+                for buf, new in ((k_buf, kn_ref), (v_buf, vn_ref)):
+                    fresh = new[new_rows, :]
+                    fresh = jnp.concatenate([fresh, fresh], axis=0)
+                    old = buf[slot, pl.ds(base, 2 * kv_heads), :].astype(F32)
+                    buf[slot, pl.ds(base, 2 * kv_heads), :] = jnp.where(mine, fresh, old).astype(BF16)
+
+    def score(j, parity):
+        b = jnp.clip(j, 0, batch - 1)
+        pieces = []
+        for h in range(2):
             for t in range(steps):
-                at = rel + t
-
-                @pl.when((at >= 0) & (at < slots))
-                def _():
-                    base = pl.multiple_of((at >> 1) * (2 * kv_heads), 2 * kv_heads)
-                    mine = upper == ((at & 1) == 1)
-                    r = t * batch + b
-                    new_rows = pl.ds((r >> 3) * (8 * kv_heads) + (r & 7), kv_heads, stride=8)
-                    for buf, new in ((k_buf, kn_ref), (v_buf, vn_ref)):
-                        fresh = new[new_rows, :]
-                        fresh = jnp.concatenate([fresh, fresh], axis=0)
-                        old = buf[slot, s, pl.ds(base, 2 * kv_heads), :].astype(F32)
-                        buf[slot, s, pl.ds(base, 2 * kv_heads), :] = jnp.where(mine, fresh, old).astype(BF16)
-
-        rels = [lens_ref[g * group + s] - first_slot for s in range(group)]
-        longest = functools.reduce(jnp.maximum, rels)
+                r = t * batch + b
+                start = (r >> 3) * (8 * heads) + (r & 7) + h * (8 * half)
+                pieces.append(q_ref[pl.ds(start, half, stride=8), :].astype(BF16))
+        query = jnp.concatenate(pieces, axis=0)
+        scores_refs[parity][...] = lax.dot_general(query, k_buf[lax.rem(b, held)], (((1,), (1,)), ((), ())), preferred_element_type=F32)
+
+    def soften(j, parity):
+        rel = rel_of(j)
+        known = (j >= 0) & (j < batch)
+        max_lane = jnp.where(known, j, 1024)
+        sum_lane = jnp.where(known, j + batch, 1024)
+        size = 16
+        block_lane = lax.broadcasted_iota(jnp.int32, (size, 128), 1)
+        for first in range(0, rows, size):
+            here = slice(first, first + size)
+            scores = jnp.where(dist[here, :] <= rel, scores_refs[parity][here, :], -jnp.inf)
+            row_max = jnp.maximum(jnp.max(scores, axis=1, keepdims=True), MASKED_MAX)
+            weights = jnp.exp2((scores - row_max) * scale)
+            row_sum = jnp.sum(weights, axis=1, keepdims=True)
+            weights_refs[parity][here, :] = weights.astype(BF16)
+            stats = jnp.where(block_lane == max_lane, row_max, stat_ref[here, :])
+            stat_ref[here, :] = jnp.where(block_lane == sum_lane, row_sum, stats)
+
+    def mix(j, parity):
+        b = jnp.clip(j, 0, batch - 1)
+        mixed = jnp.dot(weights_refs[parity][...], v_buf[lax.rem(b, held)], preferred_element_type=F32)
+        num_ref[b] = jnp.where(rel_of(j) + steps - 1 >= 0, mixed, 0.0)
+
+    def pair(k, carry):
+        first = 2 * k
+
+        @pl.when(first < batch)
+        def _():
+            receive(first)
+            receive(first + 1)
+
+        longest = functools.reduce(jnp.maximum, [rel_of(first + n) for n in range(-2, 2)])
         visible = longest + steps - 1 >= 0
 
         @pl.when(visible)
         def _():
-            stats = stat_ref[...]
-            for s in range(group):
-                b = g * group + s
-                pieces = []
-                for h in range(2):
-                    for t in range(steps):
-                        r = t * batch + b
-                        start = (r >> 3) * (8 * heads) + (r & 7) + h * (8 * half)
-                        pieces.append(q_ref[pl.ds(start, half, stride=8), :].astype(BF16))
-                query = jnp.concatenate(pieces, axis=0)
-                scores = lax.dot_general(query, k_buf[slot, s], (((1,), (1,)), ((), ())), preferred_element_type=F32)
-                scores = jnp.where(dist[...] <= rels[s], scores, -jnp.inf)
-                row_max = jnp.maximum(jnp.max(scores, axis=1, keepdims=True), MASKED_MAX)
-                weights = jnp.exp2((scores - row_max) * scale)
-                row_sum = jnp.sum(weights, axis=1, keepdims=True)
-                num_ref[b] = jnp.dot(weights.astype(BF16), v_buf[slot, s], preferred_element_type=F32)
-                stats = jnp.where(lane == b, row_max, stats)
-                stats = jnp.where(lane == b + batch, row_sum, stats)
-            stat_ref[...] = stats
+            for parity in range(2):
+                score(first + parity, parity)
+                soften(first + parity - 1, 1 - parity)
+                mix(first + parity - 2, parity)
 
         @pl.when(jnp.logical_not(visible))
         def _():
-            for s in range(group):
-                num_ref[g * group + s] = jnp.zeros((rows, HEAD_DIM), F32)
-
-        for copy in copies_out(g, slot):
-            copy.start()
-        ahead = g + depth
-        next_slot = lax.rem(ahead, slots_held)
-
-        @pl.when(ahead < groups)
+            for parity in range(2):
+                num_ref[jnp.clip(first + parity - 2, 0, batch - 1)] = jnp.zeros((rows, HEAD_DIM), F32)
+
+        @pl.when(first >= 2)
         def _():
-            @pl.when(ahead >= slots_held)
+            for n in range(2):
+                for copy in copies_out(first - 2 + n):
+                    copy.start()
+
+        for n in range(2):
+            ahead = first + depth + n
+
+            @pl.when(ahead < batch)
             def _():
-                for copy in copies_out(ahead - slots_held, next_slot):
-                    copy.wait()
-
-            for copy in copies_in(ahead, next_slot):
-                copy.start()
+                @pl.when(ahead >= held)
+                def _():
+                    for copy in copies_out(ahead - held):
+                        copy.wait()
+
+                for copy in copies_in(ahead):
+                    copy.start()
 
         return carry
 
-    lax.fori_loop(0, groups, one_group, 0)
-    for g in range(groups - slots_held, groups):
-        for copy in copies_out(g, g % slots_held):
+    lax.fori_loop(0, batch // 2 + 1, pair, 0)
+    for b in range(batch - held, batch):
+        for copy in copies_out(b):
             copy.wait()
 
 
@@ -251,18 +280,22 @@
     heads = queries.shape[1]
     rows = steps * heads
     key_rows = slots * kv_heads
-    group, depth, held = 2, 5, 8
+    depth, held = 16, 32
     cache = jax.ShapeDtypeStruct((batch, key_rows, head_dim), BF16)
     k_out, v_out, numer, stats = pl.pallas_call(
-        functools.partial(attend_kernel, steps, group, depth),
+        functools.partial(attend_kernel, steps, depth),
         name='attend',
         in_specs=[pl.BlockSpec(memory_space=pltpu.SMEM), IN_PLACE, IN_PLACE, IN_VMEM, IN_VMEM, IN_VMEM],
         out_specs=(IN_PLACE, IN_PLACE, IN_VMEM, IN_VMEM),
         out_shape=(cache, cache, jax.ShapeDtypeStruct((batch, rows, head_dim), F32), jax.ShapeDtypeStruct((rows, 128), F32)),
         scratch_shapes=[
-            VMEM((held, group, key_rows, head_dim), BF16),
-            VMEM((held, group, key_rows, head_dim), BF16),
+            VMEM((held, key_rows, head_dim), BF16),
+            VMEM((held, key_rows, head_dim), BF16),
             VMEM((rows, key_rows), jnp.int32),
+            VMEM((rows, key_rows), F32),
+            VMEM((rows, key_rows), F32),
+            VMEM((rows, key_rows), BF16),
+            VMEM((rows, key_rows), BF16),
             DMA((held, 2)),
             DMA((held, 2)),
         ],

time: 111 us -> 104 us (0.937)
  Pallas kernels: 104 us -> 96.5 us
    pallas_call x1, Pallas kernels: 35 us -> 27.2 us  [attend(): pl.pallas_call(functools.partial(attend_kernel, steps, depth), name='atte...]
where the time goes in v1:
time: 104 us; the launch traced here: 103 us
  Pallas kernels  96.5 us (93%)
  other arithmetic  4.36 us (4%)
  local copies, waits for them, and re-layouts  1.68 us (2%)
    pallas_call x1, Pallas kernels, merge(): pl.pallas_call(functools.partial(merge_kernel, chunks, steps), name='merg...  56.2 us
    pallas_call x1, Pallas kernels, attend(): pl.pallas_call(functools.partial(attend_kernel, steps, depth), name='atte...  27.2 us
    pallas_call x1, Pallas kernels, project(): pl.pallas_call(functools.partial(project_kernel, width, heads, kv_heads),...  13.1 us
    convert_element_type x1, other arithmetic, per_device(): y_steps = (x_steps.astype(F32) + (own + other)).astype(BF16)  2.28 us

profile of v1, /device:TPU:0, one launch (start us, length us, event | category | flops | bytes accessed | tf_op | source)
XLA Modules:
  0.0 103.2 jit_solution(17443329144242101447)
XLA Ops:
  0.6 0.7 add_convert_fusion.1
  1.3 0.1 convert_element_type.25
  1.4 0.7 fusion.1.gain_ref
  2.1 0.5 multiply_cosine_fusion
  2.7 0.1 maximum_maximum_fusion.rope_ref
  2.8 0.0 copy-start
  2.8 1.6 %copy-done = bf16[4,64,4096]{2,1,0:T(8,128)(2,1)S(1)} copy-done((bf16[4,64,4096]{2,1,0:T(8,128)(2,1)S(1)}, bf16[4,64,4096]{2,1,0:T(8,128)(2,1)}, u32[]{:S(2)}) %copy-start) | copy-done | bytes 2097176
  4.4 0.0 copy-start.2
  4.4 13.1 %project.1 = (f32[32,32,8,128]{3,2,1,0:T(8,128)S(1)}, f32[32,8,8,128]{3,2,1,0:T(8,128)S(1)}, f32[32,8,8,128]{3,2,1,0:T(8,128)S(1)}) custom-call(bf16[256,4096]{1,0:T(8,128)(2,1)S(1)} %bitcast.13, f32[512,128]{1,0:T(8,128)S(1)} %maximum_maximum_fusion.rope_ref, f32[34,128]{1,0:T(8,128)S(1)} %fusion.1.gain_ref, bf16[4096,4096]{1,0:T(8,128)(2,1)} %wq_hbm.1, ...), custom_call_target="tpu_custom_call" | custom-call | tf_op jit(solution)/shard_map/project/pallas_call | solution.py:117
  17.5 0.0 copy-done.2
  17.5 27.2 %attend.1 = (bf16[64,1024,128]{2,1,0:T(8,128)(2,1)}, bf16[64,1024,128]{2,1,0:T(8,128)(2,1)}, f32[64,128,128]{2,1,0:T(8,128)S(1)}, f32[128,128]{1,0:T(8,128)S(1)}) custom-call(s32[64]{0:T(128)S(1)} %copy-done.2, bf16[64,1024,128]{2,1,0:T(8,128)(2,1)} %bitcast.17, bf16[64,1024,128]{2,1,0:T(8,128)(2,1)} %bitcast.18, f32[8192,128]{1,0:T(8,128)S(1)} %bitcast.14, ...), custom_call_target="tpu_custom_call" | custom-call | tf_op jit(solution)/shard_map/attend/pallas_call | solution.py:285
  44.7 0.0 copy-start.1
  44.7 56.2 %merge.1 = (f32[4,64,4096]{2,1,0:T(8,128)S(1)}, f32[4,64,4096]{2,1,0:T(8,128)S(1)}) custom-call(f32[64,128,128]{2,1,0:T(8,128)S(1)} %get-tuple-element.15.numer, f32[128,128]{1,0:T(8,128)S(1)} %get-tuple-element.16.stats, bf16[4096,4096]{1,0:T(8,128)(2,1)} %wo_hbm.1), custom_call_target="tpu_custom_call" | custom-call | tf_op jit(solution)/shard_map/merge/pallas_call | solution.py:408
  101.0 0.0 copy-done.1
  101.0 2.3 %add_convert_fusion = bf16[4,64,4096]{2,1,0:T(8,128)(2,1)} fusion(f32[4,64,4096]{2,1,0:T(8,128)S(1)} %get-tuple-element.17, f32[4,64,4096]{2,1,0:T(8,128)S(1)} %get-tuple-element.18, bf16[4,64,4096]{2,1,0:T(8,128)(2,1)S(1)} %copy-done.1), kind=kLoop, calls=%fused_computation | loop fusion | flops 4194304 | bytes 12582912 | tf_op jit(solution)/shard_map/convert_element_type | solution.py:442
  (1 shorter events, 0.0 us)
Async XLA Ops:
  2.8 1.6 %copy-start = (bf16[4,64,4096]{2,1,0:T(8,128)(2,1)S(1)}, bf16[4,64,4096]{2,1,0:T(8,128)(2,1)}, u32[]{:S(2)}) copy-start(bf16[4,64,4096]{2,1,0:T(8,128)(2,1)} %param.11) | copy-start | bytes 6291460
  4.4 13.1 %copy-start.2 = (s32[64]{0:T(128)S(1)}, s32[64]{0:T(128)}, u32[]{:S(2)}) copy-start(s32[64]{0:T(128)} %lens_ref.1) | copy-start | bytes 772
  44.7 56.2 %copy-start.1 = (bf16[4,64,4096]{2,1,0:T(8,128)(2,1)S(1)}, bf16[4,64,4096]{2,1,0:T(8,128)(2,1)}, u32[]{:S(2)}) copy-start(bf16[4,64,4096]{2,1,0:T(8,128)(2,1)} %param.11) | copy-start | bytes 6291460

commit v2 on v1

--- a/solution.py
+++ b/solution.py
@@ -135,9 +135,10 @@
     )(x_steps.reshape(rows, hidden), rope, gains, w_q, w_k, w_v)
 
 
-def attend_kernel(steps, depth, lens_ref, k_hbm, v_hbm, q_ref, kn_ref, vn_ref, ko_hbm, vo_hbm, num_ref, stat_ref, k_buf, v_buf, dist, scores_0, scores_1, weights_0, weights_1, sems_in, sems_out):
+def attend_kernel(steps, depth, start, lens_ref, k_hbm, v_hbm, q_ref, kn_ref, vn_ref, ko_hbm, vo_hbm, num_ref, stat_ref, k_buf, v_buf, dist, scores_0, scores_1, weights_0, weights_1, sems_in, sems_out):
     held, key_rows, _ = k_buf.shape
     batch = lens_ref.shape[0]
+    count = num_ref.shape[0]
     heads, kv_heads = q_ref.shape[0] // (steps * batch), kn_ref.shape[0] // (steps * batch)
     slots = key_rows // kv_heads
     rows = steps * heads
@@ -149,13 +150,13 @@
 
     def copies_in(b):
         slot = lax.rem(b, held)
-        return (pltpu.make_async_copy(k_hbm.at[b], k_buf.at[slot], sems_in.at[slot, 0]),
-                pltpu.make_async_copy(v_hbm.at[b], v_buf.at[slot], sems_in.at[slot, 1]))
+        return (pltpu.make_async_copy(k_hbm.at[start + b], k_buf.at[slot], sems_in.at[slot, 0]),
+                pltpu.make_async_copy(v_hbm.at[start + b], v_buf.at[slot], sems_in.at[slot, 1]))
 
     def copies_out(b):
         slot = lax.rem(b, held)
-        return (pltpu.make_async_copy(k_buf.at[slot], ko_hbm.at[b], sems_out.at[slot, 0]),
-                pltpu.make_async_copy(v_buf.at[slot], vo_hbm.at[b], sems_out.at[slot, 1]))
+        return (pltpu.make_async_copy(k_buf.at[slot], ko_hbm.at[start + b], sems_out.at[slot, 0]),
+                pltpu.make_async_copy(v_buf.at[slot], vo_hbm.at[start + b], sems_out.at[slot, 1]))
 
     for b in range(depth):
         for copy in copies_in(b):
@@ -170,7 +171,7 @@
     dist[...] = jnp.where(row_kv == lax.rem(col, kv_heads), col // kv_heads - in_half // half, 1 << 24)
 
     def rel_of(b):
-        return lens_ref[jnp.clip(b, 0, batch - 1)] - first_slot
+        return lens_ref[start + jnp.clip(b, 0, count - 1)] - first_slot
 
     def receive(b):
         slot = lax.rem(b, held)
@@ -184,7 +185,7 @@
             def _():
                 base = pl.multiple_of((at >> 1) * (2 * kv_heads), 2 * kv_heads)
                 mine = upper == ((at & 1) == 1)
-                r = t * batch + b
+                r = t * batch + start + b
                 new_rows = pl.ds((r >> 3) * (8 * kv_heads) + (r & 7), kv_heads, stride=8)
                 for buf, new in ((k_buf, kn_ref), (v_buf, vn_ref)):
                     fresh = new[new_rows, :]
@@ -193,21 +194,21 @@
                     buf[slot, pl.ds(base, 2 * kv_heads), :] = jnp.where(mine, fresh, old).astype(BF16)
 
     def score(j, parity):
-        b = jnp.clip(j, 0, batch - 1)
+        b = jnp.clip(j, 0, count - 1)
         pieces = []
         for h in range(2):
             for t in range(steps):
-                r = t * batch + b
-                start = (r >> 3) * (8 * heads) + (r & 7) + h * (8 * half)
-                pieces.append(q_ref[pl.ds(start, half, stride=8), :].astype(BF16))
+                r = t * batch + start + b
+                at = (r >> 3) * (8 * heads) + (r & 7) + h * (8 * half)
+                pieces.append(q_ref[pl.ds(at, half, stride=8), :].astype(BF16))
         query = jnp.concatenate(pieces, axis=0)
         scores_refs[parity][...] = lax.dot_general(query, k_buf[lax.rem(b, held)], (((1,), (1,)), ((), ())), preferred_element_type=F32)
 
     def soften(j, parity):
         rel = rel_of(j)
-        known = (j >= 0) & (j < batch)
-        max_lane = jnp.where(known, j, 1024)
-        sum_lane = jnp.where(known, j + batch, 1024)
+        known = (j >= 0) & (j < count)
+        max_lane = jnp.where(known, start + j, 1024)
+        sum_lane = jnp.where(known, start + j + batch, 1024)
         size = 16
         block_lane = lax.broadcasted_iota(jnp.int32, (size, 128), 1)
         for first in range(0, rows, size):
@@ -221,14 +222,14 @@
             stat_ref[here, :] = jnp.where(block_lane == sum_lane, row_sum, stats)
 
     def mix(j, parity):
-        b = jnp.clip(j, 0, batch - 1)
+        b = jnp.clip(j, 0, count - 1)
         mixed = jnp.dot(weights_refs[parity][...], v_buf[lax.rem(b, held)], preferred_element_type=F32)
         num_ref[b] = jnp.where(rel_of(j) + steps - 1 >= 0, mixed, 0.0)
 
     def pair(k, carry):
         first = 2 * k
 
-        @pl.when(first < batch)
+        @pl.when(first < count)
         def _():
             receive(first)
             receive(first + 1)
@@ -246,7 +247,7 @@
         @pl.when(jnp.logical_not(visible))
         def _():
             for parity in range(2):
-                num_ref[jnp.clip(first + parity - 2, 0, batch - 1)] = jnp.zeros((rows, HEAD_DIM), F32)
+                num_ref[jnp.clip(first + parity - 2, 0, count - 1)] = jnp.zeros((rows, HEAD_DIM), F32)
 
         @pl.when(first >= 2)
         def _():
@@ -257,7 +258,7 @@
         for n in range(2):
             ahead = first + depth + n
 
-            @pl.when(ahead < batch)
+            @pl.when(ahead < count)
             def _():
                 @pl.when(ahead >= held)
                 def _():
@@ -269,25 +270,31 @@
 
         return carry
 
-    lax.fori_loop(0, batch // 2 + 1, pair, 0)
-    for b in range(batch - held, batch):
+    lax.fori_loop(0, count // 2 + 1, pair, 0)
+    for b in range(max(count - held, 0), count):
         for copy in copies_out(b):
             copy.wait()
 
 
-def attend(seq_lens, k_cache, v_cache, queries, k_new, v_new, steps):
-    batch, slots, kv_heads, head_dim = k_cache.shape
+def attend(seq_lens, k_cache, v_cache, queries, k_new, v_new, steps, start, count, partial=()):
+    batch, key_rows, head_dim = k_cache.shape
     heads = queries.shape[1]
     rows = steps * heads
-    key_rows = slots * kv_heads
     depth, held = 16, 32
-    cache = jax.ShapeDtypeStruct((batch, key_rows, head_dim), BF16)
-    k_out, v_out, numer, stats = pl.pallas_call(
-        functools.partial(attend_kernel, steps, depth),
+    cache = jax.ShapeDtypeStruct(k_cache.shape, BF16)
+    flops = 4 * count * rows * key_rows * head_dim
+    kernel = functools.partial(attend_kernel, steps, depth, start)
+
+    def continued(*refs):
+        kernel(*refs[:6], *refs[8:])
+
+    return pl.pallas_call(
+        continued if partial else kernel,
         name='attend',
-        in_specs=[pl.BlockSpec(memory_space=pltpu.SMEM), IN_PLACE, IN_PLACE, IN_VMEM, IN_VMEM, IN_VMEM],
+        in_specs=[pl.BlockSpec(memory_space=pltpu.SMEM), IN_PLACE, IN_PLACE, IN_VMEM, IN_VMEM, IN_VMEM] + [IN_PLACE] * len(partial),
         out_specs=(IN_PLACE, IN_PLACE, IN_VMEM, IN_VMEM),
-        out_shape=(cache, cache, jax.ShapeDtypeStruct((batch, rows, head_dim), F32), jax.ShapeDtypeStruct((rows, 128), F32)),
+        out_shape=(cache, cache, jax.ShapeDtypeStruct((count, rows, head_dim), F32), jax.ShapeDtypeStruct((rows, 128), F32)),
+        input_output_aliases={6: 0, 7: 1} if partial else {},
         scratch_shapes=[
             VMEM((held, key_rows, head_dim), BF16),
             VMEM((held, key_rows, head_dim), BF16),
@@ -299,22 +306,87 @@
             DMA((held, 2)),
             DMA((held, 2)),
         ],
+        cost_estimate=pl.CostEstimate(flops=flops, bytes_accessed=4 * count * key_rows * head_dim * 2, transcendentals=0),
         compiler_params=pltpu.CompilerParams(vmem_limit_bytes=32 * MIB),
-    )(seq_lens, k_cache.reshape(batch, key_rows, head_dim), v_cache.reshape(batch, key_rows, head_dim), queries.reshape(-1, head_dim), k_new.reshape(-1, head_dim), v_new.reshape(-1, head_dim))
-    return k_out.reshape(k_cache.shape), v_out.reshape(v_cache.shape), numer, stats
-
-
-def merge_kernel(chunks, steps, numer, stats, wo_hbm, y_own, y_other, wo, stat_d, stat_send, stat_x, recv_d, send_x, recv_x, scaled, att_f32, attended, sems_w, sem_stat, sems_d, sems_x, sems_y):
+    )(seq_lens, k_cache, v_cache, queries.reshape(-1, head_dim), k_new.reshape(-1, head_dim), v_new.reshape(-1, head_dim), *partial)
+
+
+def combine(mine, theirs, batch):
+    scale = HEAD_DIM ** -0.5
+    top = jnp.maximum(mine, theirs)
+    fac_a, fac_b = jnp.exp((mine - top) * scale), jnp.exp((theirs - top) * scale)
+    total = pltpu.roll(mine, 128 - batch, 1) * fac_a + pltpu.roll(theirs, 128 - batch, 1) * fac_b
+    return top, fac_a, fac_b, total
+
+
+def join_stats(top, total, batch):
+    lane = lax.broadcasted_iota(jnp.int32, top.shape, 1)
+    return jnp.where(lane < batch, top, pltpu.roll(total, batch, 1))
+
+
+def places():
+    me = lax.axis_index('sp')
+    core = lax.rem(me, 2)
+    return core, me + 1 - 2 * core, lax.rem(me + 2, 4)
+
+
+def spans(chunks):
+    return [(sum(chunks[:c]), seqs) for c, seqs in enumerate(chunks)]
+
+
+def pair_kernel(chunks, batch, numer, stats, out, stat_d, recv_d, scaled, sem_stat, sems_d):
+    rows = numer.shape[1] // 2
+    core, other_core, _ = places()
+    own = pl.ds(pl.multiple_of(core * rows, rows), rows)
+    other = pl.ds(pl.multiple_of((1 - core) * rows, rows), rows)
+    meet(other_core)
+    stat_copy = remote(stats.at[other], stat_d, sem_stat, other_core)
+    stat_copy.start()
+    copies = []
+    for c, (first, seqs) in enumerate(spans(chunks)):
+        here = pl.ds(first, seqs)
+        copy = remote(numer.at[here, other], recv_d.at[here], sems_d.at[c], other_core)
+        copy.start()
+        copies.append(copy)
+    stat_copy.wait()
+    top, fac_a, fac_b, total = combine(stats[own, :], stat_d[...], batch)
+    out[numer.shape[0]] = join_stats(top, total, batch)
+    scaled[0] = fac_a
+    scaled[1] = fac_b
+    for copy, (first, seqs) in zip(copies, spans(chunks)):
+        copy.wait()
+        for b in range(first, first + seqs):
+            out[b] = numer[b, own, :] * scaled[0, :, b:b + 1] + recv_d[b] * scaled[1, :, b:b + 1]
+
+
+def merge_pair(numer, stats, batch):
+    count, rows, _ = numer.shape
+    chunks = (8,) * (count // 8)
+    return pl.pallas_call(
+        functools.partial(pair_kernel, chunks, batch),
+        name='merge_pair',
+        out_shape=jax.ShapeDtypeStruct((count + 1, rows // 2, HEAD_DIM), F32),
+        in_specs=[IN_VMEM, IN_VMEM],
+        out_specs=IN_VMEM,
+        scratch_shapes=[
+            VMEM((rows // 2, 128), F32),
+            VMEM((count, rows // 2, HEAD_DIM), F32),
+            VMEM((2, rows // 2, 128), F32),
+            DMA((2,)),
+            DMA((len(chunks), 2)),
+        ],
+        compiler_params=pltpu.CompilerParams(collective_id=2, has_side_effects=True, vmem_limit_bytes=16 * MIB),
+    )(numer, stats)
+
+
+def merge_kernel(early_chunks, chunks, steps, numer, stats, early_own, early_theirs, wo_hbm, y_own, y_other, wo, stat_d, stat_send, stat_x, recv_d, send_x, recv_x, scaled, att_f32, attended, sems_w, sem_stat, sems_d, sems_x, sems_y):
     _, batch, hidden = y_own.shape
     rows = numer.shape[1] // 2
     half = rows // steps
-    me = lax.axis_index('sp')
-    core = lax.rem(me, 2)
-    other_core = me + 1 - 2 * core
-    other_chip = lax.rem(me + 2, 4)
+    start = batch - numer.shape[0]
+    core, other_core, other_chip = places()
     own = pl.ds(pl.multiple_of(core * rows, rows), rows)
     other = pl.ds(pl.multiple_of((1 - core) * rows, rows), rows)
-    firsts = [sum(chunks[:c]) for c in range(len(chunks))]
 
     w_pieces = sems_w.shape[0]
     w_rows = half * HEAD_DIM // w_pieces
@@ -324,7 +396,7 @@
     stat_copy = remote(stats.at[other], stat_d, sem_stat.at[0], other_core)
     stat_copy.start()
     core_copies = []
-    for c, (first, seqs) in enumerate(zip(firsts, chunks)):
+    for c, (first, seqs) in enumerate(spans(chunks)):
         here = pl.ds(first, seqs)
         copy = remote(numer.at[here, other], recv_d.at[here], sems_d.at[c], other_core)
         copy.start()
@@ -336,89 +408,94 @@
         copy.start()
         w_copies.append(copy)
 
-    lane = lax.broadcasted_iota(jnp.int32, (rows, 128), 1)
-    scale = HEAD_DIM ** -0.5
-
-    def combine(mine, theirs):
-        top = jnp.maximum(mine, theirs)
-        fac_a, fac_b = jnp.exp((mine - top) * scale), jnp.exp((theirs - top) * scale)
-        total = pltpu.roll(mine, 128 - batch, 1) * fac_a + pltpu.roll(theirs, 128 - batch, 1) * fac_b
-        return top, fac_a, fac_b, total
-
     stat_copy.wait()
-    top, fac_a, fac_b, total = combine(stats[own, :], stat_d[...])
-    stat_send[...] = jnp.where(lane < batch, top, pltpu.roll(total, batch, 1))
+    top, fac_a, fac_b, total = combine(stats[own, :], stat_d[...], batch)
+    stat_send[...] = join_stats(top, total, batch)
     scaled[0] = fac_a
     scaled[1] = fac_b
     chip_stat_copy = remote(stat_send, stat_x, sem_stat.at[1], other_chip)
     chip_stat_copy.start()
 
     chip_copies = []
-    for c, (first, seqs) in enumerate(zip(firsts, chunks)):
+    for c, (first, seqs) in enumerate(spans(chunks)):
         core_copies[c].wait()
-        for b in range(first, first + seqs):
-            send_x[b] = numer[b, own, :] * scaled[0, :, b:b + 1] + recv_d[b] * scaled[1, :, b:b + 1]
+        for i in range(first, first + seqs):
+            b = start + i
+            send_x[i] = numer[i, own, :] * scaled[0, :, b:b + 1] + recv_d[i] * scaled[1, :, b:b + 1]
         here = pl.ds(first, seqs)
         copy = remote(send_x.at[here], recv_x.at[here], sems_x.at[c], other_chip)
         copy.start()
         chip_copies.append(copy)
 
-    chip_stat_copy.wait()
-    _, fac_a, fac_b, total = combine(stat_send[...], stat_x[...])
-    scaled[0] = fac_a / total
-    scaled[1] = fac_b / total
-
     width = 512
     y_copies = []
-    for c, (first, seqs) in enumerate(zip(firsts, chunks)):
-        chip_copies[c].wait()
-        for b in range(first, first + seqs):
-            merged = send_x[b] * scaled[0, :, b:b + 1] + recv_x[b] * scaled[1, :, b:b + 1]
-            att_f32[pl.ds((b - first) * rows, rows), :] = merged
+
+    def finish(mine, theirs, first, seqs, begin):
+        for i in range(first, first + seqs):
+            b = begin + i
+            merged = mine[i] * scaled[0, :, b:b + 1] + theirs[i] * scaled[1, :, b:b + 1]
+            att_f32[pl.ds((i - first) * rows, rows), :] = merged
         for t in range(steps):
             for h in range(half):
                 values = att_f32[pl.ds(t * half + h, seqs, stride=rows), :]
                 attended[t * seqs:(t + 1) * seqs, h * HEAD_DIM:(h + 1) * HEAD_DIM] = values
-        if c == 0:
+        if not y_copies:
             for copy in w_copies:
                 copy.wait()
+        at = begin + first
 
         @pl.loop(0, hidden // width)
         def _(j):
             cols = pl.ds(pl.multiple_of(j * width, width), width)
             out = jnp.dot(attended[:steps * seqs, :].astype(BF16), wo[:, cols], preferred_element_type=F32)
             for t in range(steps):
-                y_own[t, first:first + seqs, cols] = out[t * seqs:(t + 1) * seqs, :]
-
-        here = pl.ds(first, seqs)
-        copy = remote(y_own.at[:, here, :], y_other.at[:, here, :], sems_y.at[c], other_core)
+                y_own[t, at:at + seqs, cols] = out[t * seqs:(t + 1) * seqs, :]
+
+        here = pl.ds(at, seqs)
+        copy = remote(y_own.at[:, here, :], y_other.at[:, here, :], sems_y.at[len(y_copies)], other_core)
         copy.start()
         y_copies.append(copy)
+
+    def set_factors(mine, theirs):
+        _, fac_a, fac_b, total = combine(mine, theirs, batch)
+        scaled[0] = fac_a / total
+        scaled[1] = fac_b / total
+
+    set_factors(early_own[start], early_theirs[start])
+    for first, seqs in spans(early_chunks):
+        finish(early_own, early_theirs, first, seqs, 0)
+    chip_stat_copy.wait()
+    set_factors(stat_send[...], stat_x[...])
+    for c, (first, seqs) in enumerate(spans(chunks)):
+        chip_copies[c].wait()
+        finish(send_x, recv_x, first, seqs, start)
     for copy in y_copies:
         copy.wait()
 
 
-def merge(numer, stats, w_o, steps):
-    batch, rows, _ = numer.shape
+def merge(numer, stats, early_own, early_theirs, w_o, steps, batch):
+    count, rows, _ = numer.shape
     hidden = w_o.shape[1]
-    chunks = (16, 16, 16, 8, 8)
-    largest = max(chunks)
+    early_chunks = (16, 8)
+    chunks = (8, 16, 8, 8)
+    largest = max(chunks + early_chunks)
     part = jax.ShapeDtypeStruct((steps, batch, hidden), F32)
     stat = VMEM((rows // 2, 128), F32)
+    moved = VMEM((count, rows // 2, HEAD_DIM), F32)
     return pl.pallas_call(
-        functools.partial(merge_kernel, chunks, steps),
+        functools.partial(merge_kernel, early_chunks, chunks, steps),
         name='merge',
         out_shape=(part, part),
-        in_specs=[IN_VMEM, IN_VMEM, IN_PLACE],
+        in_specs=[IN_VMEM] * 4 + [IN_PLACE],
         out_specs=(IN_VMEM, IN_VMEM),
         scratch_shapes=[
             VMEM((w_o.shape[0] // 2, hidden), BF16),
             stat,
             stat,
             stat,
-            VMEM((batch, rows // 2, HEAD_DIM), F32),
-            VMEM((batch, rows // 2, HEAD_DIM), F32),
-            VMEM((batch, rows // 2, HEAD_DIM), F32),
+            moved,
+            moved,
+            moved,
             VMEM((2, rows // 2, 128), F32),
             VMEM((largest * rows // 2, HEAD_DIM), F32),
             VMEM((steps * largest, w_o.shape[0] // 2), F32),
@@ -426,21 +503,27 @@
             DMA((2, 2)),
             DMA((len(chunks), 2)),
             DMA((len(chunks), 2)),
-            DMA((len(chunks), 2)),
+            DMA((len(chunks) + len(early_chunks), 2)),
         ],
         compiler_params=pltpu.CompilerParams(collective_id=0, has_side_effects=True, vmem_limit_bytes=40 * MIB),
-    )(numer, stats, w_o)
+    )(numer, stats, early_own, early_theirs, w_o)
 
 
 def solution(mesh):
     def per_device(x_steps, k_local, v_local, seq_lens, norm_gain, w_q, w_k, w_v, w_o, q_gain, k_gain):
-        steps = x_steps.shape[0]
+        steps, batch, _ = x_steps.shape
+        early = 24
         rope, gains = small_tables(seq_lens, steps, norm_gain, q_gain, k_gain)
-        queries, keys_new, vals_new = project(x_steps, rope, gains, w_q, w_k, w_v)
-        k_out, v_out, numer, stats = attend(seq_lens, k_local, v_local, queries, keys_new, vals_new, steps)
-        own, other = merge(numer, stats, w_o, steps)
+        fresh = project(x_steps, rope, gains, w_q, w_k, w_v)
+        flat = (batch, -1, HEAD_DIM)
+        caches = (k_local.reshape(flat), v_local.reshape(flat))
+        k_part, v_part, early_numer, early_stats = attend(seq_lens, *caches, *fresh, steps, 0, early)
+        early_own = merge_pair(early_numer, early_stats, batch)
+        early_theirs = lax.ppermute(early_own, 'sp', [(i, (i + 2) % 4) for i in range(4)])
+        k_out, v_out, numer, stats = attend(seq_lens, *caches, *fresh, steps, early, batch - early, (k_part, v_part))
+        own, other = merge(numer, stats, early_own, early_theirs, w_o, steps, batch)
         y_steps = (x_steps.astype(F32) + (own + other)).astype(BF16)
-        return y_steps, k_out, v_out
+        return y_steps, k_out.reshape(k_local.shape), v_out.reshape(v_local.shape)
 
     cache_spec = P('dp', 'sp', None, None)
     step_spec = P(None, 'dp', None)

time: 104 us -> 95.3 us (0.916)
  Pallas kernels: 96.5 us -> 86.5 us
  starting transfers between devices: 0 us -> 1.39 us
    pallas_call x2 -> x4, Pallas kernels: 83.4 us -> 73.5 us  [the longest x1 39 us: merge(): pl.pallas_call(functools.partial(merge_kernel, early_chunks, chunks, step...]
    ppermute x0 -> x1, starting transfers between devices: none -> 1.39 us  [per_device(): lax.ppermute(early_own, 'sp', [(i, (i + 2) % 4) for i in range(4)])]
  transfers between devices with their start and end apart: 0 -> 1, of which waited for: 0 -> 1; matrix products, arithmetic and copies ran while one was open for 0% -> 0% of each run, Pallas kernels for 0% -> 20%
where the time goes in v2:
time: 95.3 us; the launch traced here: 94.8 us
  Pallas kernels  86.5 us (91%)
  other arithmetic  4.36 us (5%)
  local copies, waits for them, and re-layouts  1.68 us (2%)
  starting transfers between devices  1.39 us (1%)
    pallas_call x1, Pallas kernels, merge(): pl.pallas_call(functools.partial(merge_kernel, early_chunks, chunks, step...  39 us
    pallas_call x2, Pallas kernels, attend(): pl.pallas_call(continued if partial else kernel, name='attend', in_specs=...  31.8 us
    pallas_call x1, Pallas kernels, project(): pl.pallas_call(functools.partial(project_kernel, width, heads, kv_heads),...  13.1 us
    pallas_call x1, Pallas kernels, merge_pair(): pl.pallas_call(functools.partial(pair_kernel, chunks, batch), name='merge...  2.64 us
    convert_element_type x1, other arithmetic, per_device(): y_steps = (x_steps.astype(F32) + (own + other)).astype(BF16)  2.28 us
  transfers between devices with their start and end apart: 1, of which 1 were waited for; matrix products, arithmetic and copies ran while one was open for 0% of the time, Pallas kernels for 20%

profile of v2, /device:TPU:0, one launch (start us, length us, event | category | flops | bytes accessed | tf_op | source)
XLA Modules:
  0.0 94.8 jit_solution(1130161054437094355)
XLA Ops:
  0.6 0.7 add_convert_fusion.1
  1.3 0.1 convert_element_type.25
  1.4 0.5 multiply_cosine_fusion
  1.9 0.7 fusion.1.gain_ref
  2.7 0.1 maximum_maximum_fusion.rope_ref
  2.8 0.0 copy-start
  2.8 1.6 %copy-done = bf16[4,64,4096]{2,1,0:T(8,128)(2,1)S(1)} copy-done((bf16[4,64,4096]{2,1,0:T(8,128)(2,1)S(1)}, bf16[4,64,4096]{2,1,0:T(8,128)(2,1)}, u32[]{:S(2)}) %copy-start) | copy-done | bytes 2097176
  4.4 0.0 copy-start.2
  4.4 13.1 %project.1 = (f32[32,32,8,128]{3,2,1,0:T(8,128)S(1)}, f32[32,8,8,128]{3,2,1,0:T(8,128)S(1)}, f32[32,8,8,128]{3,2,1,0:T(8,128)S(1)}) custom-call(bf16[256,4096]{1,0:T(8,128)(2,1)S(1)} %bitcast.15, f32[512,128]{1,0:T(8,128)S(1)} %maximum_maximum_fusion.rope_ref, f32[34,128]{1,0:T(8,128)S(1)} %fusion.1.gain_ref, bf16[4096,4096]{1,0:T(8,128)(2,1)} %wq_hbm.1, ...), custom_call_target="tpu_custom_call" | custom-call | tf_op jit(solution)/shard_map/project/pallas_call | solution.py:117
  17.5 0.0 copy-done.2
  17.5 13.0 %attend.2 = (bf16[64,1024,128]{2,1,0:T(8,128)(2,1)}, bf16[64,1024,128]{2,1,0:T(8,128)(2,1)}, f32[24,128,128]{2,1,0:T(8,128)S(1)}, f32[128,128]{1,0:T(8,128)S(1)}) custom-call(s32[64]{0:T(128)S(1)} %copy-done.2, bf16[64,1024,128]{2,1,0:T(8,128)(2,1)} %bitcast.20, bf16[64,1024,128]{2,1,0:T(8,128)(2,1)} %bitcast.22, f32[8192,128]{1,0:T(8,128)S(1)} %bitcast.13, ...), custom_call_target="tpu_custom_call" | custom-call | flops 1610612736 | bytes 25165824 | tf_op jit(solution)/shard_map/attend/pallas_call | solution.py:291
  30.5 2.6 %merge_pair.1.early_own = f32[25,64,128]{2,1,0:T(8,128)S(1)} custom-call(f32[24,128,128]{2,1,0:T(8,128)S(1)} %get-tuple-element.23.numer, f32[128,128]{1,0:T(8,128)S(1)} %get-tuple-element.24.stats), custom_call_target="tpu_custom_call" | custom-call | tf_op jit(solution)/shard_map/merge_pair/pallas_call | solution.py:365
  33.2 1.4 %collective-permute-start = (f32[25,64,128]{2,1,0:T(8,128)S(1)}, f32[25,64,128]{2,1,0:T(8,128)S(1)}, u32[]{:S(2)}, u32[]{:S(2)}) collective-permute-start(f32[25,64,128]{2,1,0:T(8,128)S(1)} %merge_pair.1.early_own), channel_id=1, source_target_pairs={{0,2},{1,3},{2,0},{3,1},{4,6},{5,7},{6,4},{7,5},{8,10},{9,11},{10,... | collective-permute-start | bytes 2457608 | tf_op jit(solution)/shard_map/ppermute | solution.py:522
  34.5 18.8 %attend.3 = (bf16[64,1024,128]{2,1,0:T(8,128)(2,1)}, bf16[64,1024,128]{2,1,0:T(8,128)(2,1)}, f32[40,128,128]{2,1,0:T(8,128)S(1)}, f32[128,128]{1,0:T(8,128)S(1)}) custom-call(s32[64]{0:T(128)S(1)} %copy-done.2, bf16[64,1024,128]{2,1,0:T(8,128)(2,1)} %bitcast.21, bf16[64,1024,128]{2,1,0:T(8,128)(2,1)} %bitcast.23, ...), custom_call_target="tpu_custom_call", output_to_operand_aliasing={{0}: (6, {}), {1}: (7, {})} | custom-call | flops 2684354560 | bytes 41943040 | tf_op jit(solution)/shard_map/attend/pallas_call | solution.py:291
  53.3 0.2 collective-permute-done.early_theirs
  53.5 0.0 copy-start.1
  53.5 39.0 %merge.1 = (f32[4,64,4096]{2,1,0:T(8,128)S(1)}, f32[4,64,4096]{2,1,0:T(8,128)S(1)}) custom-call(f32[40,128,128]{2,1,0:T(8,128)S(1)} %get-tuple-element.21.numer, f32[128,128]{1,0:T(8,128)S(1)} %get-tuple-element.22.stats, f32[25,64,128]{2,1,0:T(8,128)S(1)} %merge_pair.1.early_own, f32[25,64,128]{2,1,0:T(8,128)S(1)} %collective-permute-done.early_theirs, ...), custom_call_target="tpu_custom_call" | custom-call | tf_op jit(solution)/shard_map/merge/pallas_call | solution.py:485
  92.5 0.0 copy-done.1
  92.6 2.3 %add_convert_fusion = bf16[4,64,4096]{2,1,0:T(8,128)(2,1)} fusion(f32[4,64,4096]{2,1,0:T(8,128)S(1)} %get-tuple-element.25, f32[4,64,4096]{2,1,0:T(8,128)S(1)} %get-tuple-element.26, bf16[4,64,4096]{2,1,0:T(8,128)(2,1)S(1)} %copy-done.1), kind=kLoop, calls=%fused_computation | loop fusion | flops 4194304 | bytes 12582912 | tf_op jit(solution)/shard_map/convert_element_type | solution.py:525
  (1 shorter events, 0.0 us)
Async XLA Ops:
  2.8 1.6 %copy-start = (bf16[4,64,4096]{2,1,0:T(8,128)(2,1)S(1)}, bf16[4,64,4096]{2,1,0:T(8,128)(2,1)}, u32[]{:S(2)}) copy-start(bf16[4,64,4096]{2,1,0:T(8,128)(2,1)} %param.11) | copy-start | bytes 6291460
  4.4 13.1 %copy-start.2 = (s32[64]{0:T(128)S(1)}, s32[64]{0:T(128)}, u32[]{:S(2)}) copy-start(s32[64]{0:T(128)} %refs_0_.1) | copy-start | bytes 772
  33.2 20.3 %collective-permute-start = (f32[25,64,128]{2,1,0:T(8,128)S(1)}, f32[25,64,128]{2,1,0:T(8,128)S(1)}, u32[]{:S(2)}, u32[]{:S(2)}) collective-permute-start(f32[25,64,128]{2,1,0:T(8,128)S(1)} %merge_pair.1.early_own), channel_id=1, source_target_pairs={{0,2},{1,3},{2,0},{3,1},{4,6},{5,7},{6,4},{7,5},{8,10},{9,11},{10,... | collective-permute-start | bytes 2457608 | tf_op jit(solution)/shard_map/ppermute | solution.py:522
  53.5 39.1 %copy-start.1 = (bf16[4,64,4096]{2,1,0:T(8,128)(2,1)S(1)}, bf16[4,64,4096]{2,1,0:T(8,128)(2,1)}, u32[]{:S(2)}) copy-start(bf16[4,64,4096]{2,1,0:T(8,128)(2,1)} %param.11) | copy-start | bytes 6291460

commit v3 on v2

--- a/solution.py
+++ b/solution.py
@@ -132,7 +132,7 @@
             DMA((1, 2)),
         ],
         compiler_params=pltpu.CompilerParams(collective_id=1, has_side_effects=True, vmem_limit_bytes=40 * MIB),
-    )(x_steps.reshape(rows, hidden), rope, gains, w_q, w_k, w_v)
+    )(pltpu.with_memory_space_constraint(x_steps.reshape(rows, hidden), pltpu.HBM), rope, gains, w_q, w_k, w_v)
 
 
 def attend_kernel(steps, depth, start, lens_ref, k_hbm, v_hbm, q_ref, kn_ref, vn_ref, ko_hbm, vo_hbm, num_ref, stat_ref, k_buf, v_buf, dist, scores_0, scores_1, weights_0, weights_1, sems_in, sems_out):
@@ -421,54 +421,71 @@
         core_copies[c].wait()
         for i in range(first, first + seqs):
             b = start + i
-            send_x[i] = numer[i, own, :] * scaled[0, :, b:b + 1] + recv_d[i] * scaled[1, :, b:b + 1]
+            joined = numer[i, own, :] * scaled[0, :, b:b + 1] + recv_d[i] * scaled[1, :, b:b + 1]
+            send_x[i] = joined.reshape(send_x.shape[1:])
         here = pl.ds(first, seqs)
-        copy = remote(send_x.at[here], recv_x.at[here], sems_x.at[c], other_chip)
-        copy.start()
-        chip_copies.append(copy)
+        if c < len(chunks) - 1:
+            views = [(send_x.at[here], recv_x.at[here])]
+        else:
+            views = [(send_x.at[here, :, part], recv_x.at[here, :, part]) for part in range(2)]
+        for src, dst in views:
+            copy = remote(src, dst, sems_x.at[len(chip_copies)], other_chip)
+            copy.start()
+            chip_copies.append(copy)
 
     width = 512
     y_copies = []
 
-    def finish(mine, theirs, first, seqs, begin):
+    def finish(mine, theirs, first, seqs, begin, parts):
+        size = half // 2
         for i in range(first, first + seqs):
             b = begin + i
-            merged = mine[i] * scaled[0, :, b:b + 1] + theirs[i] * scaled[1, :, b:b + 1]
-            att_f32[pl.ds((i - first) * rows, rows), :] = merged
+            for t in range(steps):
+                for part in parts:
+                    at = t * half + part * size
+                    here = slice(at, at + size)
+                    merged = mine[i, t, part] * scaled[0, here, b:b + 1] + theirs[i, t, part] * scaled[1, here, b:b + 1]
+                    att_f32[pl.ds((i - first) * rows + at, size), :] = merged
         for t in range(steps):
-            for h in range(half):
+            for h in range(parts[0] * size, (parts[-1] + 1) * size):
                 values = att_f32[pl.ds(t * half + h, seqs, stride=rows), :]
                 attended[t * seqs:(t + 1) * seqs, h * HEAD_DIM:(h + 1) * HEAD_DIM] = values
         if not y_copies:
             for copy in w_copies:
                 copy.wait()
         at = begin + first
+        depth = slice(parts[0] * size * HEAD_DIM, (parts[-1] + 1) * size * HEAD_DIM)
 
         @pl.loop(0, hidden // width)
         def _(j):
             cols = pl.ds(pl.multiple_of(j * width, width), width)
-            out = jnp.dot(attended[:steps * seqs, :].astype(BF16), wo[:, cols], preferred_element_type=F32)
+            out = jnp.dot(attended[:steps * seqs, depth].astype(BF16), wo[depth, cols], preferred_element_type=F32)
             for t in range(steps):
-                y_own[t, at:at + seqs, cols] = out[t * seqs:(t + 1) * seqs, :]
-
-        here = pl.ds(at, seqs)
-        copy = remote(y_own.at[:, here, :], y_other.at[:, here, :], sems_y.at[len(y_copies)], other_core)
-        copy.start()
-        y_copies.append(copy)
+                if parts[0] == 0:
+                    y_own[t, at:at + seqs, cols] = out[t * seqs:(t + 1) * seqs, :]
+                else:
+                    y_own[t, at:at + seqs, cols] += out[t * seqs:(t + 1) * seqs, :]
+
+        if parts[-1] == 1:
+            here = pl.ds(at, seqs)
+            copy = remote(y_own.at[:, here, :], y_other.at[:, here, :], sems_y.at[len(y_copies)], other_core)
+            copy.start()
+            y_copies.append(copy)
 
     def set_factors(mine, theirs):
         _, fac_a, fac_b, total = combine(mine, theirs, batch)
         scaled[0] = fac_a / total
         scaled[1] = fac_b / total
 
-    set_factors(early_own[start], early_theirs[start])
+    set_factors(early_own[start].reshape(rows, 128), early_theirs[start].reshape(rows, 128))
     for first, seqs in spans(early_chunks):
-        finish(early_own, early_theirs, first, seqs, 0)
+        finish(early_own, early_theirs, first, seqs, 0, (0, 1))
     chip_stat_copy.wait()
     set_factors(stat_send[...], stat_x[...])
     for c, (first, seqs) in enumerate(spans(chunks)):
-        chip_copies[c].wait()
-        finish(send_x, recv_x, first, seqs, start)
+        for parts in [(0, 1)] if c < len(chunks) - 1 else [(0,), (1,)]:
+            chip_copies[c + parts[0]].wait()
+            finish(send_x, recv_x, first, seqs, start, parts)
     for copy in y_copies:
         copy.wait()
 
@@ -481,7 +498,8 @@
     largest = max(chunks + early_chunks)
     part = jax.ShapeDtypeStruct((steps, batch, hidden), F32)
     stat = VMEM((rows // 2, 128), F32)
-    moved = VMEM((count, rows // 2, HEAD_DIM), F32)
+    split = (steps, 2, rows // (4 * steps), HEAD_DIM)
+    moved = VMEM((count,) + split, F32)
     return pl.pallas_call(
         functools.partial(merge_kernel, early_chunks, chunks, steps),
         name='merge',
@@ -493,7 +511,7 @@
             stat,
             stat,
             stat,
-            moved,
+            VMEM((count, rows // 2, HEAD_DIM), F32),
             moved,
             moved,
             VMEM((2, rows // 2, 128), F32),
@@ -502,11 +520,11 @@
             DMA((8,)),
             DMA((2, 2)),
             DMA((len(chunks), 2)),
-            DMA((len(chunks), 2)),
+            DMA((len(chunks) + 1, 2)),
             DMA((len(chunks) + len(early_chunks), 2)),
         ],
         compiler_params=pltpu.CompilerParams(collective_id=0, has_side_effects=True, vmem_limit_bytes=40 * MIB),
-    )(numer, stats, early_own, early_theirs, w_o)
+    )(numer, stats, early_own.reshape((-1,) + split), early_theirs.reshape((-1,) + split), w_o)
 
 
 def solution(mesh):

time: 95.3 us -> 101 us (1.060)
  Pallas kernels: 86.5 us -> 93.4 us
  local copies, waits for them, and re-layouts: 1.68 us -> 0.09 us
  waiting for transfers between devices: 0.17 us -> 1.28 us
    pallas_call x1, Pallas kernels: 13.1 us -> 20.5 us  [project(): pl.pallas_call(functools.partial(project_kernel, width, heads, kv_heads),...]
    unnamed x6 -> x4, local copies, waits for them, and re-layouts: 1.59 us -> 0.01 us
    ppermute x1, waiting for transfers between devices: 0.17 us -> 1.28 us  [per_device(): lax.ppermute(early_own, 'sp', [(i, (i + 2) % 4) for i in range(4)])]
  transfers between devices with their start and end apart: 1 -> 1, of which waited for: 1 -> 1; matrix products, arithmetic and copies ran while one was open for 0% -> 0% of each run, Pallas kernels for 20% -> 19%
where the time goes in v3:
time: 101 us; the launch traced here: 100 us
  Pallas kernels  93.4 us (92%)
  other arithmetic  4.36 us (4%)
  waiting for transfers between devices  1.28 us (1%)
    pallas_call x1, Pallas kernels, merge(): pl.pallas_call(functools.partial(merge_kernel, early_chunks, chunks, step...  38.8 us
    pallas_call x2, Pallas kernels, attend(): pl.pallas_call(continued if partial else kernel, name='attend', in_specs=...  31.4 us
    pallas_call x1, Pallas kernels, project(): pl.pallas_call(functools.partial(project_kernel, width, heads, kv_heads),...  20.5 us
    pallas_call x1, Pallas kernels, merge_pair(): pl.pallas_call(functools.partial(pair_kernel, chunks, batch), name='merge...  2.64 us
    convert_element_type x1, other arithmetic, per_device(): y_steps = (x_steps.astype(F32) + (own + other)).astype(BF16)  2.28 us
  transfers between devices with their start and end apart: 1, of which 1 were waited for; matrix products, arithmetic and copies ran while one was open for 0% of the time, Pallas kernels for 19%

profile of v3, /device:TPU:0, one launch (start us, length us, event | category | flops | bytes accessed | tf_op | source)
XLA Modules:
  0.0 100.3 jit_solution(14359694592439657710)
XLA Ops:
  0.6 0.7 add_convert_fusion.1
  1.3 0.1 convert_element_type.25
  1.4 0.5 multiply_cosine_fusion
  1.9 0.7 fusion.1.gain_ref
  2.7 0.1 maximum_maximum_fusion.rope_ref
  2.8 0.0 copy-start
  2.8 20.5 %project.1 = (f32[32,32,8,128]{3,2,1,0:T(8,128)S(1)}, f32[32,8,8,128]{3,2,1,0:T(8,128)S(1)}, f32[32,8,8,128]{3,2,1,0:T(8,128)S(1)}) custom-call(bf16[256,4096]{1,0:T(8,128)(2,1)} %bitcast.29, f32[512,128]{1,0:T(8,128)S(1)} %maximum_maximum_fusion.rope_ref, f32[34,128]{1,0:T(8,128)S(1)} %fusion.1.gain_ref, bf16[4096,4096]{1,0:T(8,128)(2,1)} %wq_hbm.1, ...), custom_call_target="tpu_custom_call" | custom-call | tf_op jit(solution)/shard_map/project/pallas_call | solution.py:117
  23.3 0.0 copy-done
  23.3 12.9 %attend.2 = (bf16[64,1024,128]{2,1,0:T(8,128)(2,1)}, bf16[64,1024,128]{2,1,0:T(8,128)(2,1)}, f32[24,128,128]{2,1,0:T(8,128)S(1)}, f32[128,128]{1,0:T(8,128)S(1)}) custom-call(s32[64]{0:T(128)S(1)} %copy-done, bf16[64,1024,128]{2,1,0:T(8,128)(2,1)} %bitcast.23, bf16[64,1024,128]{2,1,0:T(8,128)(2,1)} %bitcast.25, f32[8192,128]{1,0:T(8,128)S(1)} %bitcast.15, ...), custom_call_target="tpu_custom_call" | custom-call | flops 1610612736 | bytes 25165824 | tf_op jit(solution)/shard_map/attend/pallas_call | solution.py:291
  36.2 2.6 %merge_pair.1 = f32[25,64,128]{2,1,0:T(8,128)S(1)} custom-call(f32[24,128,128]{2,1,0:T(8,128)S(1)} %get-tuple-element.23.numer, f32[128,128]{1,0:T(8,128)S(1)} %get-tuple-element.24.stats), custom_call_target="tpu_custom_call" | custom-call | tf_op jit(solution)/shard_map/merge_pair/pallas_call | solution.py:365
  38.9 0.5 collective-permute-start
  39.3 18.6 %attend.3 = (bf16[64,1024,128]{2,1,0:T(8,128)(2,1)}, bf16[64,1024,128]{2,1,0:T(8,128)(2,1)}, f32[40,128,128]{2,1,0:T(8,128)S(1)}, f32[128,128]{1,0:T(8,128)S(1)}) custom-call(s32[64]{0:T(128)S(1)} %copy-done, bf16[64,1024,128]{2,1,0:T(8,128)(2,1)} %bitcast.24, bf16[64,1024,128]{2,1,0:T(8,128)(2,1)} %bitcast.26, ...), custom_call_target="tpu_custom_call", output_to_operand_aliasing={{0}: (6, {}), {1}: (7, {})} | custom-call | flops 2684354560 | bytes 41943040 | tf_op jit(solution)/shard_map/attend/pallas_call | solution.py:291
  57.9 1.3 %collective-permute-done = f32[25,64,128]{2,1,0:T(8,128)S(1)} collective-permute-done((f32[25,64,128]{2,1,0:T(8,128)S(1)}, f32[25,64,128]{2,1,0:T(8,128)S(1)}, u32[]{:S(2)}, u32[]{:S(2)}) %collective-permute-start) | collective-permute-done | bytes 819232 | tf_op jit(solution)/shard_map/ppermute | solution.py:540
  59.2 0.0 copy-start.1
  59.2 38.8 %merge.1 = (f32[4,64,4096]{2,1,0:T(8,128)S(1)}, f32[4,64,4096]{2,1,0:T(8,128)S(1)}) custom-call(f32[40,128,128]{2,1,0:T(8,128)S(1)} %get-tuple-element.21.numer, f32[128,128]{1,0:T(8,128)S(1)} %get-tuple-element.22.stats, f32[25,4,2,8,128]{4,3,2,1,0:T(8,128)S(1)} %bitcast.21, f32[25,4,2,8,128]{4,3,2,1,0:T(8,128)S(1)} %bitcast.22, bf16[4096,4096]{1,0:T(8,128)(2,1)} %wo_hbm.1), custom_call_target="tpu_custom_call" | custom-call | tf_op jit(solution)/shard_map/merge/pallas_call | solution.py:503
  98.0 0.0 copy-done.1
  98.0 2.3 %add_convert_fusion = bf16[4,64,4096]{2,1,0:T(8,128)(2,1)} fusion(f32[4,64,4096]{2,1,0:T(8,128)S(1)} %get-tuple-element.25, f32[4,64,4096]{2,1,0:T(8,128)S(1)} %get-tuple-element.26, bf16[4,64,4096]{2,1,0:T(8,128)(2,1)S(1)} %copy-done.1), kind=kLoop, calls=%fused_computation | loop fusion | flops 4194304 | bytes 12582912 | tf_op jit(solution)/shard_map/convert_element_type | solution.py:543
  (1 shorter events, 0.0 us)
Async XLA Ops:
  2.8 20.5 %copy-start = (s32[64]{0:T(128)S(1)}, s32[64]{0:T(128)}, u32[]{:S(2)}) copy-start(s32[64]{0:T(128)} %refs_0_.1) | copy-start | bytes 772
  38.9 20.3 %collective-permute-start = (f32[25,64,128]{2,1,0:T(8,128)S(1)}, f32[25,64,128]{2,1,0:T(8,128)S(1)}, u32[]{:S(2)}, u32[]{:S(2)}) collective-permute-start(f32[25,64,128]{2,1,0:T(8,128)S(1)} %merge_pair.1), channel_id=1, source_target_pairs={{0,2},{1,3},{2,0},{3,1},{4,6},{5,7},{6,4},{7,5},{8,10},{9,11},{10,... | collective-permute-start | bytes 2457608 | tf_op jit(solution)/shard_map/ppermute | solution.py:540
  59.2 38.8 %copy-start.1 = (bf16[4,64,4096]{2,1,0:T(8,128)(2,1)S(1)}, bf16[4,64,4096]{2,1,0:T(8,128)(2,1)}, u32[]{:S(2)}) copy-start(bf16[4,64,4096]{2,1,0:T(8,128)(2,1)} %param.11) | copy-start | bytes 6291460

commit v4 on v3

--- a/solution.py
+++ b/solution.py
@@ -58,12 +58,12 @@
     w_copies = []
     for n, (w_hbm, _, _, total, i) in enumerate(blocks):
         cols = pl.ds(pl.multiple_of(core * (total // 2 * HEAD_DIM) + i * width, width), width)
-        copy = pltpu.make_async_copy(w_hbm.at[:, cols], wbuf.at[n], sems_w.at[n])
-        copy.start()
-        w_copies.append(copy)
-
+        w_copies.append(pltpu.make_async_copy(w_hbm.at[:, cols], wbuf.at[n], sems_w.at[n]))
+
+    w_copies[0].start()
     meet(other_core)
     x_copy.wait()
+    w_copies[1].start()
 
     @pl.loop(0, rows // 16)
     def _(i):
@@ -97,6 +97,8 @@
     sends = []
     for n in range(len(blocks)):
         w_copies[n].wait()
+        if n + 2 < len(blocks):
+            w_copies[n + 2].start()
         acc[n % 2] = jnp.dot(normed[...], wbuf[n], preferred_element_type=F32)
         if n > 0:
             finish(n - 1)
@@ -280,7 +282,7 @@
     batch, key_rows, head_dim = k_cache.shape
     heads = queries.shape[1]
     rows = steps * heads
-    depth, held = 16, 32
+    depth, held = 8, 32
     cache = jax.ShapeDtypeStruct(k_cache.shape, BF16)
     flops = 4 * count * rows * key_rows * head_dim
     kernel = functools.partial(attend_kernel, steps, depth, start)
@@ -456,21 +458,25 @@
         at = begin + first
         depth = slice(parts[0] * size * HEAD_DIM, (parts[-1] + 1) * size * HEAD_DIM)
 
-        @pl.loop(0, hidden // width)
-        def _(j):
-            cols = pl.ds(pl.multiple_of(j * width, width), width)
-            out = jnp.dot(attended[:steps * seqs, depth].astype(BF16), wo[depth, cols], preferred_element_type=F32)
-            for t in range(steps):
-                if parts[0] == 0:
-                    y_own[t, at:at + seqs, cols] = out[t * seqs:(t + 1) * seqs, :]
-                else:
-                    y_own[t, at:at + seqs, cols] += out[t * seqs:(t + 1) * seqs, :]
-
-        if parts[-1] == 1:
-            here = pl.ds(at, seqs)
-            copy = remote(y_own.at[:, here, :], y_other.at[:, here, :], sems_y.at[len(y_copies)], other_core)
-            copy.start()
-            y_copies.append(copy)
+        here = pl.ds(at, seqs)
+        span = hidden // 2
+        for side in range(2):
+
+            @pl.loop(side * span // width, (side + 1) * span // width)
+            def _(j):
+                cols = pl.ds(pl.multiple_of(j * width, width), width)
+                out = jnp.dot(attended[:steps * seqs, depth].astype(BF16), wo[depth, cols], preferred_element_type=F32)
+                for t in range(steps):
+                    if parts[0] == 0:
+                        y_own[t, at:at + seqs, cols] = out[t * seqs:(t + 1) * seqs, :]
+                    else:
+                        y_own[t, at:at + seqs, cols] += out[t * seqs:(t + 1) * seqs, :]
+
+            if parts[-1] == 1:
+                lanes = pl.ds(side * span, span)
+                copy = remote(y_own.at[:, here, lanes], y_other.at[:, here, lanes], sems_y.at[len(y_copies)], other_core)
+                copy.start()
+                y_copies.append(copy)
 
     def set_factors(mine, theirs):
         _, fac_a, fac_b, total = combine(mine, theirs, batch)
@@ -494,7 +500,7 @@
     count, rows, _ = numer.shape
     hidden = w_o.shape[1]
     early_chunks = (16, 8)
-    chunks = (8, 16, 8, 8)
+    chunks = (8, 16, 16)
     largest = max(chunks + early_chunks)
     part = jax.ShapeDtypeStruct((steps, batch, hidden), F32)
     stat = VMEM((rows // 2, 128), F32)
@@ -521,7 +527,7 @@
             DMA((2, 2)),
             DMA((len(chunks), 2)),
             DMA((len(chunks) + 1, 2)),
-            DMA((len(chunks) + len(early_chunks), 2)),
+            DMA((2 * (len(chunks) + len(early_chunks)), 2)),
         ],
         compiler_params=pltpu.CompilerParams(collective_id=0, has_side_effects=True, vmem_limit_bytes=40 * MIB),
     )(numer, stats, early_own.reshape((-1,) + split), early_theirs.reshape((-1,) + split), w_o)

time: 101 us -> 94.1 us (0.932)
  Pallas kernels: 93.4 us -> 86.4 us
  starting transfers between devices: 0.47 us -> 1.99 us
  waiting for transfers between devices: 1.28 us -> 0.05 us
    pallas_call x1, Pallas kernels: 20.5 us -> 14.4 us  [project(): pl.pallas_call(functools.partial(project_kernel, width, heads, kv_heads),...]
    ppermute x1, starting transfers between devices: 0.47 us -> 1.99 us  [per_device(): lax.ppermute(early_own, 'sp', [(i, (i + 2) % 4) for i in range(4)])]
    ppermute x1, waiting for transfers between devices: 1.28 us -> 0.05 us  [per_device(): lax.ppermute(early_own, 'sp', [(i, (i + 2) % 4) for i in range(4)])]
  transfers between devices with their start and end apart: 1 -> 1, of which waited for: 1 -> 1; matrix products, arithmetic and copies ran while one was open for 0% -> 0% of each run, Pallas kernels for 19% -> 20%
where the time goes in v4:
time: 94.1 us; the launch traced here: 93.6 us
  Pallas kernels  86.4 us (92%)
  other arithmetic  4.36 us (5%)
  starting transfers between devices  1.99 us (2%)
    pallas_call x1, Pallas kernels, merge(): pl.pallas_call(functools.partial(merge_kernel, early_chunks, chunks, step...  37.8 us
    pallas_call x2, Pallas kernels, attend(): pl.pallas_call(continued if partial else kernel, name='attend', in_specs=...  31.6 us
    pallas_call x1, Pallas kernels, project(): pl.pallas_call(functools.partial(project_kernel, width, heads, kv_heads),...  14.4 us
    pallas_call x1, Pallas kernels, merge_pair(): pl.pallas_call(functools.partial(pair_kernel, chunks, batch), name='merge...  2.64 us
    convert_element_type x1, other arithmetic, per_device(): y_steps = (x_steps.astype(F32) + (own + other)).astype(BF16)  2.28 us
    ppermute x1, starting transfers between devices, per_device(): lax.ppermute(early_own, 'sp', [(i, (i + 2) % 4) for i in range(4)])  1.99 us
  transfers between devices with their start and end apart: 1, of which 1 were waited for; matrix products, arithmetic and copies ran while one was open for 0% of the time, Pallas kernels for 20%

profile of v4, /device:TPU:0, one launch (start us, length us, event | category | flops | bytes accessed | tf_op | source)
XLA Modules:
  0.0 93.6 jit_solution(6978795308692917407)
XLA Ops:
  0.6 0.7 add_convert_fusion.1
  1.3 0.1 convert_element_type.25
  1.4 0.5 multiply_cosine_fusion
  1.9 0.7 fusion.1.gain_ref
  2.7 0.1 maximum_maximum_fusion.rope_ref
  2.8 0.0 copy-start
  2.8 14.4 %project.1 = (f32[32,32,8,128]{3,2,1,0:T(8,128)S(1)}, f32[32,8,8,128]{3,2,1,0:T(8,128)S(1)}, f32[32,8,8,128]{3,2,1,0:T(8,128)S(1)}) custom-call(bf16[256,4096]{1,0:T(8,128)(2,1)} %bitcast.29, f32[512,128]{1,0:T(8,128)S(1)} %maximum_maximum_fusion.rope_ref, f32[34,128]{1,0:T(8,128)S(1)} %fusion.1.gain_ref, bf16[4096,4096]{1,0:T(8,128)(2,1)} %wq_hbm.1, ...), custom_call_target="tpu_custom_call" | custom-call | tf_op jit(solution)/shard_map/project/pallas_call | solution.py:119
  17.2 0.0 copy-done
  17.2 12.9 %attend.2 = (bf16[64,1024,128]{2,1,0:T(8,128)(2,1)}, bf16[64,1024,128]{2,1,0:T(8,128)(2,1)}, f32[24,128,128]{2,1,0:T(8,128)S(1)}, f32[128,128]{1,0:T(8,128)S(1)}) custom-call(s32[64]{0:T(128)S(1)} %copy-done, bf16[64,1024,128]{2,1,0:T(8,128)(2,1)} %bitcast.23, bf16[64,1024,128]{2,1,0:T(8,128)(2,1)} %bitcast.25, f32[8192,128]{1,0:T(8,128)S(1)} %bitcast.15, ...), custom_call_target="tpu_custom_call" | custom-call | flops 1610612736 | bytes 25165824 | tf_op jit(solution)/shard_map/attend/pallas_call | solution.py:293
  30.1 2.6 %merge_pair.1 = f32[25,64,128]{2,1,0:T(8,128)S(1)} custom-call(f32[24,128,128]{2,1,0:T(8,128)S(1)} %get-tuple-element.23.numer, f32[128,128]{1,0:T(8,128)S(1)} %get-tuple-element.24.stats), custom_call_target="tpu_custom_call" | custom-call | tf_op jit(solution)/shard_map/merge_pair/pallas_call | solution.py:367
  32.8 2.0 %collective-permute-start = (f32[25,64,128]{2,1,0:T(8,128)S(1)}, f32[25,64,128]{2,1,0:T(8,128)S(1)}, u32[]{:S(2)}, u32[]{:S(2)}) collective-permute-start(f32[25,64,128]{2,1,0:T(8,128)S(1)} %merge_pair.1), channel_id=1, source_target_pairs={{0,2},{1,3},{2,0},{3,1},{4,6},{5,7},{6,4},{7,5},{8,10},{9,11},{10,... | collective-permute-start | bytes 2457608 | tf_op jit(solution)/shard_map/ppermute | solution.py:546
  34.8 18.7 %attend.3 = (bf16[64,1024,128]{2,1,0:T(8,128)(2,1)}, bf16[64,1024,128]{2,1,0:T(8,128)(2,1)}, f32[40,128,128]{2,1,0:T(8,128)S(1)}, f32[128,128]{1,0:T(8,128)S(1)}) custom-call(s32[64]{0:T(128)S(1)} %copy-done, bf16[64,1024,128]{2,1,0:T(8,128)(2,1)} %bitcast.24, bf16[64,1024,128]{2,1,0:T(8,128)(2,1)} %bitcast.26, ...), custom_call_target="tpu_custom_call", output_to_operand_aliasing={{0}: (6, {}), {1}: (7, {})} | custom-call | flops 2684354560 | bytes 41943040 | tf_op jit(solution)/shard_map/attend/pallas_call | solution.py:293
  53.5 0.1 collective-permute-done
  53.5 0.0 copy-start.1
  53.5 37.8 %merge.1 = (f32[4,64,4096]{2,1,0:T(8,128)S(1)}, f32[4,64,4096]{2,1,0:T(8,128)S(1)}) custom-call(f32[40,128,128]{2,1,0:T(8,128)S(1)} %get-tuple-element.21.numer, f32[128,128]{1,0:T(8,128)S(1)} %get-tuple-element.22.stats, f32[25,4,2,8,128]{4,3,2,1,0:T(8,128)S(1)} %bitcast.21, f32[25,4,2,8,128]{4,3,2,1,0:T(8,128)S(1)} %bitcast.22, bf16[4096,4096]{1,0:T(8,128)(2,1)} %wo_hbm.1), custom_call_target="tpu_custom_call" | custom-call | tf_op jit(solution)/shard_map/merge/pallas_call | solution.py:509
  91.3 0.0 copy-done.1
  91.3 2.3 %add_convert_fusion = bf16[4,64,4096]{2,1,0:T(8,128)(2,1)} fusion(f32[4,64,4096]{2,1,0:T(8,128)S(1)} %get-tuple-element.25, f32[4,64,4096]{2,1,0:T(8,128)S(1)} %get-tuple-element.26, bf16[4,64,4096]{2,1,0:T(8,128)(2,1)S(1)} %copy-done.1), kind=kLoop, calls=%fused_computation | loop fusion | flops 4194304 | bytes 12582912 | tf_op jit(solution)/shard_map/convert_element_type | solution.py:549
  (1 shorter events, 0.0 us)
Async XLA Ops:
  2.8 14.4 %copy-start = (s32[64]{0:T(128)S(1)}, s32[64]{0:T(128)}, u32[]{:S(2)}) copy-start(s32[64]{0:T(128)} %refs_0_.1) | copy-start | bytes 772
  32.8 20.8 %collective-permute-start = (f32[25,64,128]{2,1,0:T(8,128)S(1)}, f32[25,64,128]{2,1,0:T(8,128)S(1)}, u32[]{:S(2)}, u32[]{:S(2)}) collective-permute-start(f32[25,64,128]{2,1,0:T(8,128)S(1)} %merge_pair.1), channel_id=1, source_target_pairs={{0,2},{1,3},{2,0},{3,1},{4,6},{5,7},{6,4},{7,5},{8,10},{9,11},{10,... | collective-permute-start | bytes 2457608 | tf_op jit(solution)/shard_map/ppermute | solution.py:546
  53.5 37.8 %copy-start.1 = (bf16[4,64,4096]{2,1,0:T(8,128)(2,1)S(1)}, bf16[4,64,4096]{2,1,0:T(8,128)(2,1)}, u32[]{:S(2)}) copy-start(bf16[4,64,4096]{2,1,0:T(8,128)(2,1)} %param.11) | copy-start | bytes 6291460

commit v5 on v4

--- a/solution.py
+++ b/solution.py
@@ -65,7 +65,7 @@
     x_copy.wait()
     w_copies[1].start()
 
-    @pl.loop(0, rows // 16)
+    @pl.loop(0, rows // 16, unroll=4)
     def _(i):
         here = pl.ds(pl.multiple_of(i * 16, 16), 16)
         values = x_rows[here, :].astype(F32)
@@ -160,7 +160,7 @@
         return (pltpu.make_async_copy(k_buf.at[slot], ko_hbm.at[start + b], sems_out.at[slot, 0]),
                 pltpu.make_async_copy(v_buf.at[slot], vo_hbm.at[start + b], sems_out.at[slot, 1]))
 
-    for b in range(depth):
+    for b in range(depth // 2):
         for copy in copies_in(b):
             copy.start()
 
@@ -236,6 +236,12 @@
             receive(first)
             receive(first + 1)
 
+        @pl.when(first == 0)
+        def _():
+            for b in range(depth // 2, depth):
+                for copy in copies_in(b):
+                    copy.start()
+
         longest = functools.reduce(jnp.maximum, [rel_of(first + n) for n in range(-2, 2)])
         visible = longest + steps - 1 >= 0
 
@@ -251,10 +257,10 @@
             for parity in range(2):
                 num_ref[jnp.clip(first + parity - 2, 0, count - 1)] = jnp.zeros((rows, HEAD_DIM), F32)
 
-        @pl.when(first >= 2)
+        @pl.when(first < count)
         def _():
             for n in range(2):
-                for copy in copies_out(first - 2 + n):
+                for copy in copies_out(first + n):
                     copy.start()
 
         for n in range(2):
@@ -282,7 +288,7 @@
     batch, key_rows, head_dim = k_cache.shape
     heads = queries.shape[1]
     rows = steps * heads
-    depth, held = 8, 32
+    depth, held = 16, 32
     cache = jax.ShapeDtypeStruct(k_cache.shape, BF16)
     flops = 4 * count * rows * key_rows * head_dim
     kernel = functools.partial(attend_kernel, steps, depth, start)

time: 94.1 us -> 92.2 us (0.980)
  Pallas kernels: 86.4 us -> 85 us
    pallas_call x1, Pallas kernels: 14.4 us -> 13.4 us  [project(): pl.pallas_call(functools.partial(project_kernel, width, heads, kv_heads),...]
  transfers between devices with their start and end apart: 1 -> 1, of which waited for: 1 -> 0; matrix products, arithmetic and copies ran while one was open for 0% -> 0% of each run, Pallas kernels for 20% -> 20%
where the time goes in v5:
time: 92.2 us
  Pallas kernels  85 us (92%)
  other arithmetic  4.36 us (5%)
  starting transfers between devices  1.98 us (2%)
    pallas_call x1, Pallas kernels, merge(): pl.pallas_call(functools.partial(merge_kernel, early_chunks, chunks, step...  37.8 us
    pallas_call x2, Pallas kernels, attend(): pl.pallas_call(continued if partial else kernel, name='attend', in_specs=...  31.2 us
    pallas_call x1, Pallas kernels, project(): pl.pallas_call(functools.partial(project_kernel, width, heads, kv_heads),...  13.4 us
    pallas_call x1, Pallas kernels, merge_pair(): pl.pallas_call(functools.partial(pair_kernel, chunks, batch), name='merge...  2.64 us
    convert_element_type x1, other arithmetic, per_device(): y_steps = (x_steps.astype(F32) + (own + other)).astype(BF16)  2.28 us
    ppermute x1, starting transfers between devices, per_device(): lax.ppermute(early_own, 'sp', [(i, (i + 2) % 4) for i in range(4)])  1.98 us
  transfers between devices with their start and end apart: 1, of which 0 were waited for; matrix products, arithmetic and copies ran while one was open for 0% of the time, Pallas kernels for 20%

profile of v5, /device:TPU:0, one launch (start us, length us, event | category | flops | bytes accessed | tf_op | source)
XLA Modules:
  0.0 92.2 jit_solution(9806616813980932632)
XLA Ops:
  0.6 0.7 add_convert_fusion.1
  1.3 0.1 convert_element_type.25
  1.4 0.5 multiply_cosine_fusion
  1.9 0.7 fusion.1.gain_ref
  2.7 0.1 maximum_maximum_fusion.rope_ref
  2.8 0.0 copy-start
  2.8 13.4 %project.1 = (f32[32,32,8,128]{3,2,1,0:T(8,128)S(1)}, f32[32,8,8,128]{3,2,1,0:T(8,128)S(1)}, f32[32,8,8,128]{3,2,1,0:T(8,128)S(1)}) custom-call(bf16[256,4096]{1,0:T(8,128)(2,1)} %bitcast.29, f32[512,128]{1,0:T(8,128)S(1)} %maximum_maximum_fusion.rope_ref, f32[34,128]{1,0:T(8,128)S(1)} %fusion.1.gain_ref, bf16[4096,4096]{1,0:T(8,128)(2,1)} %wq_hbm.1, ...), custom_call_target="tpu_custom_call" | custom-call | tf_op jit(solution)/shard_map/project/pallas_call | solution.py:119
  16.3 0.0 copy-done
  16.3 12.5 %attend.2 = (bf16[64,1024,128]{2,1,0:T(8,128)(2,1)}, bf16[64,1024,128]{2,1,0:T(8,128)(2,1)}, f32[24,128,128]{2,1,0:T(8,128)S(1)}, f32[128,128]{1,0:T(8,128)S(1)}) custom-call(s32[64]{0:T(128)S(1)} %copy-done, bf16[64,1024,128]{2,1,0:T(8,128)(2,1)} %bitcast.23, bf16[64,1024,128]{2,1,0:T(8,128)(2,1)} %bitcast.25, f32[8192,128]{1,0:T(8,128)S(1)} %bitcast.15, ...), custom_call_target="tpu_custom_call" | custom-call | flops 1610612736 | bytes 25165824 | tf_op jit(solution)/shard_map/attend/pallas_call | solution.py:299
  28.8 2.6 %merge_pair.1 = f32[25,64,128]{2,1,0:T(8,128)S(1)} custom-call(f32[24,128,128]{2,1,0:T(8,128)S(1)} %get-tuple-element.23.numer, f32[128,128]{1,0:T(8,128)S(1)} %get-tuple-element.24.stats), custom_call_target="tpu_custom_call" | custom-call | tf_op jit(solution)/shard_map/merge_pair/pallas_call | solution.py:373
  31.4 2.0 %collective-permute-start = (f32[25,64,128]{2,1,0:T(8,128)S(1)}, f32[25,64,128]{2,1,0:T(8,128)S(1)}, u32[]{:S(2)}, u32[]{:S(2)}) collective-permute-start(f32[25,64,128]{2,1,0:T(8,128)S(1)} %merge_pair.1), channel_id=1, source_target_pairs={{0,2},{1,3},{2,0},{3,1},{4,6},{5,7},{6,4},{7,5},{8,10},{9,11},{10,... | collective-permute-start | bytes 2457608 | tf_op jit(solution)/shard_map/ppermute | solution.py:552
  33.4 18.7 %attend.3 = (bf16[64,1024,128]{2,1,0:T(8,128)(2,1)}, bf16[64,1024,128]{2,1,0:T(8,128)(2,1)}, f32[40,128,128]{2,1,0:T(8,128)S(1)}, f32[128,128]{1,0:T(8,128)S(1)}) custom-call(s32[64]{0:T(128)S(1)} %copy-done, bf16[64,1024,128]{2,1,0:T(8,128)(2,1)} %bitcast.24, bf16[64,1024,128]{2,1,0:T(8,128)(2,1)} %bitcast.26, ...), custom_call_target="tpu_custom_call", output_to_operand_aliasing={{0}: (6, {}), {1}: (7, {})} | custom-call | flops 2684354560 | bytes 41943040 | tf_op jit(solution)/shard_map/attend/pallas_call | solution.py:299
  52.1 0.0 collective-permute-done
  52.1 0.0 copy-start.1
  52.1 37.8 %merge.1 = (f32[4,64,4096]{2,1,0:T(8,128)S(1)}, f32[4,64,4096]{2,1,0:T(8,128)S(1)}) custom-call(f32[40,128,128]{2,1,0:T(8,128)S(1)} %get-tuple-element.21.numer, f32[128,128]{1,0:T(8,128)S(1)} %get-tuple-element.22.stats, f32[25,4,2,8,128]{4,3,2,1,0:T(8,128)S(1)} %bitcast.21, f32[25,4,2,8,128]{4,3,2,1,0:T(8,128)S(1)} %bitcast.22, bf16[4096,4096]{1,0:T(8,128)(2,1)} %wo_hbm.1), custom_call_target="tpu_custom_call" | custom-call | tf_op jit(solution)/shard_map/merge/pallas_call | solution.py:515
  89.9 0.0 copy-done.1
  89.9 2.3 %add_convert_fusion = bf16[4,64,4096]{2,1,0:T(8,128)(2,1)} fusion(f32[4,64,4096]{2,1,0:T(8,128)S(1)} %get-tuple-element.25, f32[4,64,4096]{2,1,0:T(8,128)S(1)} %get-tuple-element.26, bf16[4,64,4096]{2,1,0:T(8,128)(2,1)S(1)} %copy-done.1), kind=kLoop, calls=%fused_computation | loop fusion | flops 4194304 | bytes 12582912 | tf_op jit(solution)/shard_map/convert_element_type | solution.py:555
  (1 shorter events, 0.0 us)
Async XLA Ops:
  2.8 13.4 %copy-start = (s32[64]{0:T(128)S(1)}, s32[64]{0:T(128)}, u32[]{:S(2)}) copy-start(s32[64]{0:T(128)} %refs_0_.1) | copy-start | bytes 772
  31.4 20.7 %collective-permute-start = (f32[25,64,128]{2,1,0:T(8,128)S(1)}, f32[25,64,128]{2,1,0:T(8,128)S(1)}, u32[]{:S(2)}, u32[]{:S(2)}) collective-permute-start(f32[25,64,128]{2,1,0:T(8,128)S(1)} %merge_pair.1), channel_id=1, source_target_pairs={{0,2},{1,3},{2,0},{3,1},{4,6},{5,7},{6,4},{7,5},{8,10},{9,11},{10,... | collective-permute-start | bytes 2457608 | tf_op jit(solution)/shard_map/ppermute | solution.py:552
  52.1 37.8 %copy-start.1 = (bf16[4,64,4096]{2,1,0:T(8,128)(2,1)S(1)}, bf16[4,64,4096]{2,1,0:T(8,128)(2,1)}, u32[]{:S(2)}) copy-start(bf16[4,64,4096]{2,1,0:T(8,128)(2,1)} %param.11) | copy-start | bytes 6291460

commit v6 on v5

--- a/solution.py
+++ b/solution.py
@@ -21,16 +21,14 @@
 IN_PLACE = pl.BlockSpec(memory_space=pl.ANY)
 
 
-def small_tables(seq_lens, steps, norm_gain, q_gain, k_gain):
+def rope_table(seq_lens, steps):
     half = HEAD_DIM // 2
     positions = (seq_lens[None, :] + jnp.arange(steps, dtype=jnp.int32)[:, None]).reshape(-1)
     inv_freq = jnp.exp(jnp.arange(half, dtype=F32) * (-2.0 * math.log(ROPE_BASE) / HEAD_DIM))
     angles = positions.astype(F32)[:, None] * inv_freq
     cosine = jnp.cos(angles)
     sine = jnp.sin(angles)
-    rope = jnp.concatenate([jnp.concatenate([cosine, cosine], axis=-1), jnp.concatenate([-sine, sine], axis=-1)], axis=0)
-    gains = jnp.concatenate([norm_gain, q_gain, k_gain]).astype(F32).reshape(-1, HEAD_DIM)
-    return rope, gains
+    return jnp.concatenate([jnp.concatenate([cosine, cosine], axis=-1), jnp.concatenate([-sine, sine], axis=-1)], axis=0)
 
 
 def remote(src, dst, sems, peer):
@@ -44,7 +42,7 @@
     pl.semaphore_wait(barrier, len(peers))
 
 
-def project_kernel(width, heads, kv_heads, x_hbm, rope_ref, gain_ref, wq_hbm, wk_hbm, wv_hbm, q_ref, k_ref, v_ref, x_rows, normed, acc, wbuf, sem_x, sems_w, sems_q, sems_k, sems_v):
+def project_kernel(width, heads, kv_heads, x_hbm, norm_hbm, q_gain_hbm, k_gain_hbm, rope_ref, wq_hbm, wk_hbm, wv_hbm, q_ref, k_ref, v_ref, x_rows, norm_rows, q_gain, k_gain, gain_ref, normed, acc, wbuf, sem_x, sems_gain, sems_w, sems_q, sems_k, sems_v):
     rows, hidden = x_rows.shape
     per_block = width // HEAD_DIM
     core = lax.rem(lax.axis_index('sp'), 2)
@@ -52,6 +50,11 @@
 
     x_copy = pltpu.make_async_copy(x_hbm, x_rows, sem_x)
     x_copy.start()
+    gain_copies = []
+    for n, (src, dst) in enumerate(((norm_hbm, norm_rows), (q_gain_hbm, q_gain), (k_gain_hbm, k_gain))):
+        copy = pltpu.make_async_copy(src, dst, sems_gain.at[n])
+        copy.start()
+        gain_copies.append(copy)
     blocks = [(wk_hbm, k_ref, sems_k, kv_heads, 0)]
     blocks += [(wq_hbm, q_ref, sems_q, heads, i) for i in range(heads // 2 // per_block)]
     blocks += [(wv_hbm, v_ref, sems_v, kv_heads, 0)]
@@ -62,6 +65,12 @@
 
     w_copies[0].start()
     meet(other_core)
+    for copy in gain_copies:
+        copy.wait()
+    norm_count = hidden // HEAD_DIM
+    gain_ref[:norm_count, :] = norm_rows[...].astype(F32)
+    gain_ref[norm_count:norm_count + 1, :] = q_gain[...].astype(F32)
+    gain_ref[norm_count + 1:norm_count + 2, :] = k_gain[...].astype(F32)
     x_copy.wait()
     w_copies[1].start()
 
@@ -109,32 +118,39 @@
         copy.wait()
 
 
-def project(x_steps, rope, gains, w_q, w_k, w_v):
+def project(x_steps, norm_gain, q_gain, k_gain, rope, w_q, w_k, w_v):
     steps, batch, hidden = x_steps.shape
     rows = steps * batch
     heads = w_q.shape[1] // HEAD_DIM
     kv_heads = w_k.shape[1] // HEAD_DIM
     width = kv_heads // 2 * HEAD_DIM
     q_blocks = heads // kv_heads
+    pinned = [x_steps.reshape(rows, hidden)] + [gain.reshape(-1, HEAD_DIM) for gain in (norm_gain, q_gain, k_gain)]
+    pinned = [pltpu.with_memory_space_constraint(array, pltpu.HBM) for array in pinned]
     return pl.pallas_call(
         functools.partial(project_kernel, width, heads, kv_heads),
         name='project',
         out_shape=tuple(jax.ShapeDtypeStruct((rows // 8, n, 8, HEAD_DIM), F32) for n in (heads, kv_heads, kv_heads)),
-        in_specs=[pl.BlockSpec(memory_space=pltpu.HBM), IN_VMEM, IN_VMEM] + [IN_PLACE] * 3,
+        in_specs=[pl.BlockSpec(memory_space=pltpu.HBM)] * 4 + [IN_VMEM] + [IN_PLACE] * 3,
         out_specs=(IN_VMEM,) * 3,
         scratch_shapes=[
             VMEM((rows, hidden), BF16),
+            VMEM((hidden // HEAD_DIM, HEAD_DIM), BF16),
+            VMEM((1, HEAD_DIM), BF16),
+            VMEM((1, HEAD_DIM), BF16),
+            VMEM((hidden // HEAD_DIM + 2, HEAD_DIM), F32),
             VMEM((rows, hidden), BF16),
             VMEM((2, rows, width), F32),
             VMEM((q_blocks + 2, hidden, width), BF16),
             DMA,
+            DMA((3,)),
             DMA((q_blocks + 2,)),
             DMA((q_blocks, 2)),
             DMA((1, 2)),
             DMA((1, 2)),
         ],
         compiler_params=pltpu.CompilerParams(collective_id=1, has_side_effects=True, vmem_limit_bytes=40 * MIB),
-    )(pltpu.with_memory_space_constraint(x_steps.reshape(rows, hidden), pltpu.HBM), rope, gains, w_q, w_k, w_v)
+    )(*pinned, rope, w_q, w_k, w_v)
 
 
 def attend_kernel(steps, depth, start, lens_ref, k_hbm, v_hbm, q_ref, kn_ref, vn_ref, ko_hbm, vo_hbm, num_ref, stat_ref, k_buf, v_buf, dist, scores_0, scores_1, weights_0, weights_1, sems_in, sems_out):
@@ -160,7 +176,7 @@
         return (pltpu.make_async_copy(k_buf.at[slot], ko_hbm.at[start + b], sems_out.at[slot, 0]),
                 pltpu.make_async_copy(v_buf.at[slot], vo_hbm.at[start + b], sems_out.at[slot, 1]))
 
-    for b in range(depth // 2):
+    for b in range(2):
         for copy in copies_in(b):
             copy.start()
 
@@ -171,6 +187,9 @@
     row_half, in_half = row // (steps * half), lax.rem(row, steps * half)
     row_kv = (row_half * half + lax.rem(in_half, half)) // (heads // kv_heads)
     dist[...] = jnp.where(row_kv == lax.rem(col, kv_heads), col // kv_heads - in_half // half, 1 << 24)
+    for b in range(2, depth // 2):
+        for copy in copies_in(b):
+            copy.start()
 
     def rel_of(b):
         return lens_ref[start + jnp.clip(b, 0, count - 1)] - first_slot
@@ -465,8 +484,8 @@
         depth = slice(parts[0] * size * HEAD_DIM, (parts[-1] + 1) * size * HEAD_DIM)
 
         here = pl.ds(at, seqs)
-        span = hidden // 2
-        for side in range(2):
+        span = hidden // 4
+        for side in range(4):
 
             @pl.loop(side * span // width, (side + 1) * span // width)
             def _(j):
@@ -533,7 +552,7 @@
             DMA((2, 2)),
             DMA((len(chunks), 2)),
             DMA((len(chunks) + 1, 2)),
-            DMA((2 * (len(chunks) + len(early_chunks)), 2)),
+            DMA((4 * (len(chunks) + len(early_chunks)), 2)),
         ],
         compiler_params=pltpu.CompilerParams(collective_id=0, has_side_effects=True, vmem_limit_bytes=40 * MIB),
     )(numer, stats, early_own.reshape((-1,) + split), early_theirs.reshape((-1,) + split), w_o)
@@ -543,8 +562,7 @@
     def per_device(x_steps, k_local, v_local, seq_lens, norm_gain, w_q, w_k, w_v, w_o, q_gain, k_gain):
         steps, batch, _ = x_steps.shape
         early = 24
-        rope, gains = small_tables(seq_lens, steps, norm_gain, q_gain, k_gain)
-        fresh = project(x_steps, rope, gains, w_q, w_k, w_v)
+        fresh = project(x_steps, norm_gain, q_gain, k_gain, rope_table(seq_lens, steps), w_q, w_k, w_v)
         flat = (batch, -1, HEAD_DIM)
         caches = (k_local.reshape(flat), v_local.reshape(flat))
         k_part, v_part, early_numer, early_stats = attend(seq_lens, *caches, *fresh, steps, 0, early)

time: 92.2 us -> 91.7 us (level)
  no operation moved by 1% of the time
where the time goes in v6:
time: 91.7 us; the launch traced here: 91.4 us
  Pallas kernels  84.9 us (93%)
  other arithmetic  3.63 us (4%)
  starting transfers between devices  2.04 us (2%)
    pallas_call x1, Pallas kernels, merge(): pl.pallas_call(functools.partial(merge_kernel, early_chunks, chunks, step...  37.6 us
    pallas_call x2, Pallas kernels, attend(): pl.pallas_call(continued if partial else kernel, name='attend', in_specs=...  31.2 us
    pallas_call x1, Pallas kernels, project(): pl.pallas_call(functools.partial(project_kernel, width, heads, kv_heads),...  13.5 us
    pallas_call x1, Pallas kernels, merge_pair(): pl.pallas_call(functools.partial(pair_kernel, chunks, batch), name='merge...  2.64 us
    convert_element_type x1, other arithmetic, per_device(): y_steps = (x_steps.astype(F32) + (own + other)).astype(BF16)  2.28 us
    ppermute x1, starting transfers between devices, per_device(): lax.ppermute(early_own, 'sp', [(i, (i + 2) % 4) for i in range(4)])  2.04 us
  transfers between devices with their start and end apart: 1, of which 0 were waited for; matrix products, arithmetic and copies ran while one was open for 0% of the time, Pallas kernels for 20%

profile of v6, /device:TPU:0, one launch (start us, length us, event | category | flops | bytes accessed | tf_op | source)
XLA Modules:
  0.0 91.4 jit_solution(1390731222915502501)
XLA Ops:
  0.6 0.7 add_convert_fusion.1
  1.3 0.1 convert_element_type.18
  1.4 0.5 multiply_cosine_fusion
  1.9 0.1 maximum_maximum_fusion.rope_ref
  2.1 0.0 copy-start
  2.1 13.5 %project.1 = (f32[32,32,8,128]{3,2,1,0:T(8,128)S(1)}, f32[32,8,8,128]{3,2,1,0:T(8,128)S(1)}, f32[32,8,8,128]{3,2,1,0:T(8,128)S(1)}) custom-call(bf16[256,4096]{1,0:T(8,128)(2,1)} %bitcast.27, bf16[32,128]{1,0:T(8,128)(2,1)} %bitcast.28, bf16[1,128]{1,0:T(2,128)(2,1)} %bitcast.29, bf16[1,128]{1,0:T(2,128)(2,1)} %bitcast.30, ...), custom_call_target="tpu_custom_call" | custom-call | tf_op jit(solution)/shard_map/project/pallas_call | solution.py:130
  15.6 0.0 copy-done
  15.6 12.5 %attend.2 = (bf16[64,1024,128]{2,1,0:T(8,128)(2,1)}, bf16[64,1024,128]{2,1,0:T(8,128)(2,1)}, f32[24,128,128]{2,1,0:T(8,128)S(1)}, f32[128,128]{1,0:T(8,128)S(1)}) custom-call(s32[64]{0:T(128)S(1)} %copy-done, bf16[64,1024,128]{2,1,0:T(8,128)(2,1)} %bitcast.21, bf16[64,1024,128]{2,1,0:T(8,128)(2,1)} %bitcast.23, f32[8192,128]{1,0:T(8,128)S(1)} %bitcast.13, ...), custom_call_target="tpu_custom_call" | custom-call | flops 1610612736 | bytes 25165824 | tf_op jit(solution)/shard_map/attend/pallas_call | solution.py:318
  28.1 2.6 %merge_pair.1 = f32[25,64,128]{2,1,0:T(8,128)S(1)} custom-call(f32[24,128,128]{2,1,0:T(8,128)S(1)} %get-tuple-element.23.numer, f32[128,128]{1,0:T(8,128)S(1)} %get-tuple-element.24.stats), custom_call_target="tpu_custom_call" | custom-call | tf_op jit(solution)/shard_map/merge_pair/pallas_call | solution.py:392
  30.8 2.0 %collective-permute-start = (f32[25,64,128]{2,1,0:T(8,128)S(1)}, f32[25,64,128]{2,1,0:T(8,128)S(1)}, u32[]{:S(2)}, u32[]{:S(2)}) collective-permute-start(f32[25,64,128]{2,1,0:T(8,128)S(1)} %merge_pair.1), channel_id=1, source_target_pairs={{0,2},{1,3},{2,0},{3,1},{4,6},{5,7},{6,4},{7,5},{8,10},{9,11},{10,... | collective-permute-start | bytes 2457608 | tf_op jit(solution)/shard_map/ppermute | solution.py:570
  32.8 18.7 %attend.3 = (bf16[64,1024,128]{2,1,0:T(8,128)(2,1)}, bf16[64,1024,128]{2,1,0:T(8,128)(2,1)}, f32[40,128,128]{2,1,0:T(8,128)S(1)}, f32[128,128]{1,0:T(8,128)S(1)}) custom-call(s32[64]{0:T(128)S(1)} %copy-done, bf16[64,1024,128]{2,1,0:T(8,128)(2,1)} %bitcast.22, bf16[64,1024,128]{2,1,0:T(8,128)(2,1)} %bitcast.24, ...), custom_call_target="tpu_custom_call", output_to_operand_aliasing={{0}: (6, {}), {1}: (7, {})} | custom-call | flops 2684354560 | bytes 41943040 | tf_op jit(solution)/shard_map/attend/pallas_call | solution.py:318
  51.5 0.0 collective-permute-done
  51.5 0.0 copy-start.1
  51.6 37.6 %merge.1 = (f32[4,64,4096]{2,1,0:T(8,128)S(1)}, f32[4,64,4096]{2,1,0:T(8,128)S(1)}) custom-call(f32[40,128,128]{2,1,0:T(8,128)S(1)} %get-tuple-element.21.numer, f32[128,128]{1,0:T(8,128)S(1)} %get-tuple-element.22.stats, f32[25,4,2,8,128]{4,3,2,1,0:T(8,128)S(1)} %bitcast.19, f32[25,4,2,8,128]{4,3,2,1,0:T(8,128)S(1)} %bitcast.20, bf16[4096,4096]{1,0:T(8,128)(2,1)} %wo_hbm.1), custom_call_target="tpu_custom_call" | custom-call | tf_op jit(solution)/shard_map/merge/pallas_call | solution.py:534
  89.1 0.0 copy-done.1
  89.1 2.3 %add_convert_fusion = bf16[4,64,4096]{2,1,0:T(8,128)(2,1)} fusion(f32[4,64,4096]{2,1,0:T(8,128)S(1)} %get-tuple-element.25, f32[4,64,4096]{2,1,0:T(8,128)S(1)} %get-tuple-element.26, bf16[4,64,4096]{2,1,0:T(8,128)(2,1)S(1)} %copy-done.1), kind=kLoop, calls=%fused_computation | loop fusion | flops 4194304 | bytes 12582912 | tf_op jit(solution)/shard_map/convert_element_type | solution.py:573
  (1 shorter events, 0.0 us)
Async XLA Ops:
  2.1 13.5 %copy-start = (s32[64]{0:T(128)S(1)}, s32[64]{0:T(128)}, u32[]{:S(2)}) copy-start(s32[64]{0:T(128)} %refs_0_.1) | copy-start | bytes 772
  30.8 20.8 %collective-permute-start = (f32[25,64,128]{2,1,0:T(8,128)S(1)}, f32[25,64,128]{2,1,0:T(8,128)S(1)}, u32[]{:S(2)}, u32[]{:S(2)}) collective-permute-start(f32[25,64,128]{2,1,0:T(8,128)S(1)} %merge_pair.1), channel_id=1, source_target_pairs={{0,2},{1,3},{2,0},{3,1},{4,6},{5,7},{6,4},{7,5},{8,10},{9,11},{10,... | collective-permute-start | bytes 2457608 | tf_op jit(solution)/shard_map/ppermute | solution.py:570
  51.5 37.6 %copy-start.1 = (bf16[4,64,4096]{2,1,0:T(8,128)(2,1)S(1)}, bf16[4,64,4096]{2,1,0:T(8,128)(2,1)}, u32[]{:S(2)}) copy-start(bf16[4,64,4096]{2,1,0:T(8,128)(2,1)} %param.11) | copy-start | bytes 6291460

commit v7 on v6

--- a/solution.py
+++ b/solution.py
@@ -21,14 +21,22 @@
 IN_PLACE = pl.BlockSpec(memory_space=pl.ANY)
 
 
-def rope_table(seq_lens, steps):
+def fill_rope_table(lens_ref, rope, steps):
     half = HEAD_DIM // 2
-    positions = (seq_lens[None, :] + jnp.arange(steps, dtype=jnp.int32)[:, None]).reshape(-1)
-    inv_freq = jnp.exp(jnp.arange(half, dtype=F32) * (-2.0 * math.log(ROPE_BASE) / HEAD_DIM))
-    angles = positions.astype(F32)[:, None] * inv_freq
-    cosine = jnp.cos(angles)
-    sine = jnp.sin(angles)
-    return jnp.concatenate([jnp.concatenate([cosine, cosine], axis=-1), jnp.concatenate([-sine, sine], axis=-1)], axis=0)
+    batch = lens_ref.shape[0]
+    shape = (batch, HEAD_DIM)
+    row = lax.broadcasted_iota(jnp.int32, shape, 0)
+    lane = lax.broadcasted_iota(jnp.int32, shape, 1)
+    lengths = jnp.zeros(shape, jnp.int32)
+    for b in range(batch):
+        lengths = jnp.where(row == b, lens_ref[b], lengths)
+    index = jnp.where(lane < half, lane, lane - half).astype(F32)
+    inv_freq = jnp.exp(index * (-2.0 * math.log(ROPE_BASE) / HEAD_DIM))
+    sign = jnp.where(lane < half, -1.0, 1.0)
+    for t in range(steps):
+        angles = (lengths + t).astype(F32) * inv_freq
+        rope[t * batch:(t + 1) * batch, :] = jnp.cos(angles)
+        rope[(steps + t) * batch:(steps + t + 1) * batch, :] = sign * jnp.sin(angles)
 
 
 def remote(src, dst, sems, peer):
@@ -42,7 +50,7 @@
     pl.semaphore_wait(barrier, len(peers))
 
 
-def project_kernel(width, heads, kv_heads, x_hbm, norm_hbm, q_gain_hbm, k_gain_hbm, rope_ref, wq_hbm, wk_hbm, wv_hbm, q_ref, k_ref, v_ref, x_rows, norm_rows, q_gain, k_gain, gain_ref, normed, acc, wbuf, sem_x, sems_gain, sems_w, sems_q, sems_k, sems_v):
+def project_kernel(width, heads, kv_heads, steps, lens_hbm, x_hbm, norm_hbm, q_gain_hbm, k_gain_hbm, wq_hbm, wk_hbm, wv_hbm, q_ref, k_ref, v_ref, x_rows, lens_ref, norm_rows, q_gain, k_gain, gain_ref, rope_ref, normed, acc, wbuf, sem_x, sems_gain, sems_w, sems_q, sems_k, sems_v):
     rows, hidden = x_rows.shape
     per_block = width // HEAD_DIM
     core = lax.rem(lax.axis_index('sp'), 2)
@@ -51,7 +59,7 @@
     x_copy = pltpu.make_async_copy(x_hbm, x_rows, sem_x)
     x_copy.start()
     gain_copies = []
-    for n, (src, dst) in enumerate(((norm_hbm, norm_rows), (q_gain_hbm, q_gain), (k_gain_hbm, k_gain))):
+    for n, (src, dst) in enumerate(((lens_hbm, lens_ref), (norm_hbm, norm_rows), (q_gain_hbm, q_gain), (k_gain_hbm, k_gain))):
         copy = pltpu.make_async_copy(src, dst, sems_gain.at[n])
         copy.start()
         gain_copies.append(copy)
@@ -71,6 +79,7 @@
     gain_ref[:norm_count, :] = norm_rows[...].astype(F32)
     gain_ref[norm_count:norm_count + 1, :] = q_gain[...].astype(F32)
     gain_ref[norm_count + 1:norm_count + 2, :] = k_gain[...].astype(F32)
+    fill_rope_table(lens_ref, rope_ref, steps)
     x_copy.wait()
     w_copies[1].start()
 
@@ -118,39 +127,41 @@
         copy.wait()
 
 
-def project(x_steps, norm_gain, q_gain, k_gain, rope, w_q, w_k, w_v):
+def project(seq_lens, x_steps, norm_gain, q_gain, k_gain, w_q, w_k, w_v):
     steps, batch, hidden = x_steps.shape
     rows = steps * batch
     heads = w_q.shape[1] // HEAD_DIM
     kv_heads = w_k.shape[1] // HEAD_DIM
     width = kv_heads // 2 * HEAD_DIM
     q_blocks = heads // kv_heads
-    pinned = [x_steps.reshape(rows, hidden)] + [gain.reshape(-1, HEAD_DIM) for gain in (norm_gain, q_gain, k_gain)]
+    pinned = [seq_lens, x_steps.reshape(rows, hidden)] + [gain.reshape(-1, HEAD_DIM) for gain in (norm_gain, q_gain, k_gain)]
     pinned = [pltpu.with_memory_space_constraint(array, pltpu.HBM) for array in pinned]
     return pl.pallas_call(
-        functools.partial(project_kernel, width, heads, kv_heads),
+        functools.partial(project_kernel, width, heads, kv_heads, steps),
         name='project',
         out_shape=tuple(jax.ShapeDtypeStruct((rows // 8, n, 8, HEAD_DIM), F32) for n in (heads, kv_heads, kv_heads)),
-        in_specs=[pl.BlockSpec(memory_space=pltpu.HBM)] * 4 + [IN_VMEM] + [IN_PLACE] * 3,
+        in_specs=[pl.BlockSpec(memory_space=pltpu.HBM)] * 5 + [IN_PLACE] * 3,
         out_specs=(IN_VMEM,) * 3,
         scratch_shapes=[
             VMEM((rows, hidden), BF16),
+            pltpu.SMEM(seq_lens.shape, jnp.int32),
             VMEM((hidden // HEAD_DIM, HEAD_DIM), BF16),
             VMEM((1, HEAD_DIM), BF16),
             VMEM((1, HEAD_DIM), BF16),
             VMEM((hidden // HEAD_DIM + 2, HEAD_DIM), F32),
+            VMEM((2 * rows, HEAD_DIM), F32),
             VMEM((rows, hidden), BF16),
             VMEM((2, rows, width), F32),
             VMEM((q_blocks + 2, hidden, width), BF16),
             DMA,
-            DMA((3,)),
+            DMA((4,)),
             DMA((q_blocks + 2,)),
             DMA((q_blocks, 2)),
             DMA((1, 2)),
             DMA((1, 2)),
         ],
         compiler_params=pltpu.CompilerParams(collective_id=1, has_side_effects=True, vmem_limit_bytes=40 * MIB),
-    )(*pinned, rope, w_q, w_k, w_v)
+    )(*pinned, w_q, w_k, w_v)
 
 
 def attend_kernel(steps, depth, start, lens_ref, k_hbm, v_hbm, q_ref, kn_ref, vn_ref, ko_hbm, vo_hbm, num_ref, stat_ref, k_buf, v_buf, dist, scores_0, scores_1, weights_0, weights_1, sems_in, sems_out):
@@ -562,7 +573,7 @@
     def per_device(x_steps, k_local, v_local, seq_lens, norm_gain, w_q, w_k, w_v, w_o, q_gain, k_gain):
         steps, batch, _ = x_steps.shape
         early = 24
-        fresh = project(x_steps, norm_gain, q_gain, k_gain, rope_table(seq_lens, steps), w_q, w_k, w_v)
+        fresh = project(seq_lens, x_steps, norm_gain, q_gain, k_gain, w_q, w_k, w_v)
         flat = (batch, -1, HEAD_DIM)
         caches = (k_local.reshape(flat), v_local.reshape(flat))
         k_part, v_part, early_numer, early_stats = attend(seq_lens, *caches, *fresh, steps, 0, early)

time: 91.7 us -> 89.9 us (0.980)
  other arithmetic: 3.63 us -> 2.28 us
  transfers between devices with their start and end apart: 1 -> 1, of which waited for: 0 -> 0; matrix products, arithmetic and copies ran while one was open for 0% -> 0% of each run, Pallas kernels for 20% -> 21%
where the time goes in v7:
time: 89.9 us; the launch traced here: 90 us
  Pallas kernels  84.8 us (94%)
  other arithmetic  2.28 us (3%)
  starting transfers between devices  2.16 us (2%)
    pallas_call x1, Pallas kernels, merge(): pl.pallas_call(functools.partial(merge_kernel, early_chunks, chunks, step...  37.6 us
    pallas_call x2, Pallas kernels, attend(): pl.pallas_call(continued if partial else kernel, name='attend', in_specs=...  31.1 us
    pallas_call x1, Pallas kernels, project(): pl.pallas_call(functools.partial(project_kernel, width, heads, kv_heads,...  13.5 us
    pallas_call x1, Pallas kernels, merge_pair(): pl.pallas_call(functools.partial(pair_kernel, chunks, batch), name='merge...  2.63 us
    convert_element_type x1, other arithmetic, per_device(): y_steps = (x_steps.astype(F32) + (own + other)).astype(BF16)  2.28 us
    ppermute x1, starting transfers between devices, per_device(): lax.ppermute(early_own, 'sp', [(i, (i + 2) % 4) for i in range(4)])  2.16 us
  transfers between devices with their start and end apart: 1, of which 0 were waited for; matrix products, arithmetic and copies ran while one was open for 0% of the time, Pallas kernels for 21%

profile of v7, /device:TPU:0, one launch (start us, length us, event | category | flops | bytes accessed | tf_op | source)
XLA Modules:
  0.0 90.0 jit_solution(11957950993574767129)
XLA Ops:
  0.6 0.0 copy-start
  0.6 13.5 %project.1 = (f32[32,32,8,128]{3,2,1,0:T(8,128)S(1)}, f32[32,8,8,128]{3,2,1,0:T(8,128)S(1)}, f32[32,8,8,128]{3,2,1,0:T(8,128)S(1)}) custom-call(s32[64]{0:T(128)} %refs_0_.1, bf16[256,4096]{1,0:T(8,128)(2,1)} %bitcast.27, bf16[32,128]{1,0:T(8,128)(2,1)} %bitcast.28, bf16[1,128]{1,0:T(2,128)(2,1)} %bitcast.29, bf16[1,128]{1,0:T(2,128)(2,1)} %bitcast.30, ...), custom_call_target="tpu_custom_call" | custom-call | tf_op jit(solution)/shard_map/project/pallas_call | solution.py:139
  14.2 0.0 copy-done
  14.2 12.5 %attend.2 = (bf16[64,1024,128]{2,1,0:T(8,128)(2,1)}, bf16[64,1024,128]{2,1,0:T(8,128)(2,1)}, f32[24,128,128]{2,1,0:T(8,128)S(1)}, f32[128,128]{1,0:T(8,128)S(1)}) custom-call(s32[64]{0:T(128)S(1)} %copy-done, bf16[64,1024,128]{2,1,0:T(8,128)(2,1)} %bitcast.21, bf16[64,1024,128]{2,1,0:T(8,128)(2,1)} %bitcast.23, f32[8192,128]{1,0:T(8,128)S(1)} %bitcast.13, ...), custom_call_target="tpu_custom_call" | custom-call | flops 1610612736 | bytes 25165824 | tf_op jit(solution)/shard_map/attend/pallas_call | solution.py:329
  26.7 2.6 %merge_pair.1 = f32[25,64,128]{2,1,0:T(8,128)S(1)} custom-call(f32[24,128,128]{2,1,0:T(8,128)S(1)} %get-tuple-element.23.numer, f32[128,128]{1,0:T(8,128)S(1)} %get-tuple-element.24.stats), custom_call_target="tpu_custom_call" | custom-call | tf_op jit(solution)/shard_map/merge_pair/pallas_call | solution.py:403
  29.3 2.2 %collective-permute-start = (f32[25,64,128]{2,1,0:T(8,128)S(1)}, f32[25,64,128]{2,1,0:T(8,128)S(1)}, u32[]{:S(2)}, u32[]{:S(2)}) collective-permute-start(f32[25,64,128]{2,1,0:T(8,128)S(1)} %merge_pair.1), channel_id=1, source_target_pairs={{0,2},{1,3},{2,0},{3,1},{4,6},{5,7},{6,4},{7,5},{8,10},{9,11},{10,... | collective-permute-start | bytes 2457608 | tf_op jit(solution)/shard_map/ppermute | solution.py:581
  31.5 18.6 %attend.3 = (bf16[64,1024,128]{2,1,0:T(8,128)(2,1)}, bf16[64,1024,128]{2,1,0:T(8,128)(2,1)}, f32[40,128,128]{2,1,0:T(8,128)S(1)}, f32[128,128]{1,0:T(8,128)S(1)}) custom-call(s32[64]{0:T(128)S(1)} %copy-done, bf16[64,1024,128]{2,1,0:T(8,128)(2,1)} %bitcast.22, bf16[64,1024,128]{2,1,0:T(8,128)(2,1)} %bitcast.24, ...), custom_call_target="tpu_custom_call", output_to_operand_aliasing={{0}: (6, {}), {1}: (7, {})} | custom-call | flops 2684354560 | bytes 41943040 | tf_op jit(solution)/shard_map/attend/pallas_call | solution.py:329
  50.1 0.0 collective-permute-done
  50.1 0.0 copy-start.1
  50.1 37.6 %merge.1 = (f32[4,64,4096]{2,1,0:T(8,128)S(1)}, f32[4,64,4096]{2,1,0:T(8,128)S(1)}) custom-call(f32[40,128,128]{2,1,0:T(8,128)S(1)} %get-tuple-element.21.numer, f32[128,128]{1,0:T(8,128)S(1)} %get-tuple-element.22.stats, f32[25,4,2,8,128]{4,3,2,1,0:T(8,128)S(1)} %bitcast.19, f32[25,4,2,8,128]{4,3,2,1,0:T(8,128)S(1)} %bitcast.20, bf16[4096,4096]{1,0:T(8,128)(2,1)} %wo_hbm.1), custom_call_target="tpu_custom_call" | custom-call | tf_op jit(solution)/shard_map/merge/pallas_call | solution.py:545
  87.7 0.0 copy-done.1
  87.7 2.3 %add_convert_fusion = bf16[4,64,4096]{2,1,0:T(8,128)(2,1)} fusion(f32[4,64,4096]{2,1,0:T(8,128)S(1)} %get-tuple-element.25, f32[4,64,4096]{2,1,0:T(8,128)S(1)} %get-tuple-element.26, bf16[4,64,4096]{2,1,0:T(8,128)(2,1)S(1)} %copy-done.1), kind=kLoop, calls=%fused_computation | loop fusion | flops 4194304 | bytes 12582912 | tf_op jit(solution)/shard_map/convert_element_type | solution.py:584
Async XLA Ops:
  0.6 13.5 %copy-start = (s32[64]{0:T(128)S(1)}, s32[64]{0:T(128)}, u32[]{:S(2)}) copy-start(s32[64]{0:T(128)} %refs_0_.1) | copy-start | bytes 772
  29.3 20.8 %collective-permute-start = (f32[25,64,128]{2,1,0:T(8,128)S(1)}, f32[25,64,128]{2,1,0:T(8,128)S(1)}, u32[]{:S(2)}, u32[]{:S(2)}) collective-permute-start(f32[25,64,128]{2,1,0:T(8,128)S(1)} %merge_pair.1), channel_id=1, source_target_pairs={{0,2},{1,3},{2,0},{3,1},{4,6},{5,7},{6,4},{7,5},{8,10},{9,11},{10,... | collective-permute-start | bytes 2457608 | tf_op jit(solution)/shard_map/ppermute | solution.py:581
  50.1 37.6 %copy-start.1 = (bf16[4,64,4096]{2,1,0:T(8,128)(2,1)S(1)}, bf16[4,64,4096]{2,1,0:T(8,128)(2,1)}, u32[]{:S(2)}) copy-start(bf16[4,64,4096]{2,1,0:T(8,128)(2,1)} %param.11) | copy-start | bytes 6291460

commit v8 on v7

--- a/solution.py
+++ b/solution.py
@@ -50,14 +50,20 @@
     pl.semaphore_wait(barrier, len(peers))
 
 
-def project_kernel(width, heads, kv_heads, steps, lens_hbm, x_hbm, norm_hbm, q_gain_hbm, k_gain_hbm, wq_hbm, wk_hbm, wv_hbm, q_ref, k_ref, v_ref, x_rows, lens_ref, norm_rows, q_gain, k_gain, gain_ref, rope_ref, normed, acc, wbuf, sem_x, sems_gain, sems_w, sems_q, sems_k, sems_v):
+def project_kernel(width, heads, kv_heads, steps, lens_hbm, x_hbm, norm_hbm, q_gain_hbm, k_gain_hbm, wq_hbm, wk_hbm, wv_hbm, q_ref, k_ref, v_ref, x_rows, lens_ref, norm_rows, q_gain, k_gain, gain_ref, rope_ref, normed, acc, wbuf, sems_x, sems_gain, sems_w, sems_q, sems_k, sems_v):
     rows, hidden = x_rows.shape
     per_block = width // HEAD_DIM
     core = lax.rem(lax.axis_index('sp'), 2)
     other_core = lax.axis_index('sp') + 1 - 2 * core
 
-    x_copy = pltpu.make_async_copy(x_hbm, x_rows, sem_x)
-    x_copy.start()
+    pieces = sems_x.shape[0]
+    piece = rows // pieces
+    x_copies = []
+    for n in range(pieces):
+        here = pl.ds(n * piece, piece)
+        copy = pltpu.make_async_copy(x_hbm.at[here], x_rows.at[here], sems_x.at[n])
+        copy.start()
+        x_copies.append(copy)
     gain_copies = []
     for n, (src, dst) in enumerate(((lens_hbm, lens_ref), (norm_hbm, norm_rows), (q_gain_hbm, q_gain), (k_gain_hbm, k_gain))):
         copy = pltpu.make_async_copy(src, dst, sems_gain.at[n])
@@ -80,17 +86,21 @@
     gain_ref[norm_count:norm_count + 1, :] = q_gain[...].astype(F32)
     gain_ref[norm_count + 1:norm_count + 2, :] = k_gain[...].astype(F32)
     fill_rope_table(lens_ref, rope_ref, steps)
-    x_copy.wait()
-    w_copies[1].start()
-
-    @pl.loop(0, rows // 16, unroll=4)
-    def _(i):
-        here = pl.ds(pl.multiple_of(i * 16, 16), 16)
-        values = x_rows[here, :].astype(F32)
-        inv_rms = lax.rsqrt(jnp.mean(values * values, axis=-1, keepdims=True) + NORM_EPS)
-        for n in range(hidden // HEAD_DIM):
-            lanes = slice(n * HEAD_DIM, (n + 1) * HEAD_DIM)
-            normed[here, lanes] = (x_rows[here, lanes].astype(F32) * inv_rms * gain_ref[n:n + 1, :]).astype(BF16)
+    def norm_piece(first):
+        @pl.loop(0, piece // 16, unroll=4)
+        def _(i):
+            here = pl.ds(pl.multiple_of(first + i * 16, 16), 16)
+            values = x_rows[here, :].astype(F32)
+            inv_rms = lax.rsqrt(jnp.mean(values * values, axis=-1, keepdims=True) + NORM_EPS)
+            for n in range(hidden // HEAD_DIM):
+                lanes = slice(n * HEAD_DIM, (n + 1) * HEAD_DIM)
+                normed[here, lanes] = (x_rows[here, lanes].astype(F32) * inv_rms * gain_ref[n:n + 1, :]).astype(BF16)
+
+    for n in range(pieces):
+        x_copies[n].wait()
+        if n == 0:
+            w_copies[1].start()
+        norm_piece(n * piece)
 
     def finish(n):
         w_hbm, out_ref, sems, total, i = blocks[n]
@@ -153,7 +163,7 @@
             VMEM((rows, hidden), BF16),
             VMEM((2, rows, width), F32),
             VMEM((q_blocks + 2, hidden, width), BF16),
-            DMA,
+            DMA((4,)),
             DMA((4,)),
             DMA((q_blocks + 2,)),
             DMA((q_blocks, 2)),

time: 89.9 us -> 90 us (level)
  no operation moved by 1% of the time
where the time goes in v8:
time: 90 us; the launch traced here: 89.9 us
  Pallas kernels  85 us (94%)
  other arithmetic  2.28 us (3%)
  starting transfers between devices  1.97 us (2%)
    pallas_call x1, Pallas kernels, merge(): pl.pallas_call(functools.partial(merge_kernel, early_chunks, chunks, step...  37.6 us
    pallas_call x2, Pallas kernels, attend(): pl.pallas_call(continued if partial else kernel, name='attend', in_specs=...  31.2 us
    pallas_call x1, Pallas kernels, project(): pl.pallas_call(functools.partial(project_kernel, width, heads, kv_heads,...  13.5 us
    pallas_call x1, Pallas kernels, merge_pair(): pl.pallas_call(functools.partial(pair_kernel, chunks, batch), name='merge...  2.63 us
    convert_element_type x1, other arithmetic, per_device(): y_steps = (x_steps.astype(F32) + (own + other)).astype(BF16)  2.28 us
    ppermute x1, starting transfers between devices, per_device(): lax.ppermute(early_own, 'sp', [(i, (i + 2) % 4) for i in range(4)])  1.97 us
  transfers between devices with their start and end apart: 1, of which 0 were waited for; matrix products, arithmetic and copies ran while one was open for 0% of the time, Pallas kernels for 21%

profile of v8, /device:TPU:0, one launch (start us, length us, event | category | flops | bytes accessed | tf_op | source)
XLA Modules:
  0.0 89.9 jit_solution(2606986061518835070)
XLA Ops:
  0.6 0.0 copy-start
  0.6 13.5 %project.1 = (f32[32,32,8,128]{3,2,1,0:T(8,128)S(1)}, f32[32,8,8,128]{3,2,1,0:T(8,128)S(1)}, f32[32,8,8,128]{3,2,1,0:T(8,128)S(1)}) custom-call(s32[64]{0:T(128)} %refs_0_.1, bf16[256,4096]{1,0:T(8,128)(2,1)} %bitcast.27, bf16[32,128]{1,0:T(8,128)(2,1)} %bitcast.28, bf16[1,128]{1,0:T(2,128)(2,1)} %bitcast.29, bf16[1,128]{1,0:T(2,128)(2,1)} %bitcast.30, ...), custom_call_target="tpu_custom_call" | custom-call | tf_op jit(solution)/shard_map/project/pallas_call | solution.py:149
  14.2 0.0 copy-done
  14.2 12.6 %attend.2 = (bf16[64,1024,128]{2,1,0:T(8,128)(2,1)}, bf16[64,1024,128]{2,1,0:T(8,128)(2,1)}, f32[24,128,128]{2,1,0:T(8,128)S(1)}, f32[128,128]{1,0:T(8,128)S(1)}) custom-call(s32[64]{0:T(128)S(1)} %copy-done, bf16[64,1024,128]{2,1,0:T(8,128)(2,1)} %bitcast.21, bf16[64,1024,128]{2,1,0:T(8,128)(2,1)} %bitcast.23, f32[8192,128]{1,0:T(8,128)S(1)} %bitcast.13, ...), custom_call_target="tpu_custom_call" | custom-call | flops 1610612736 | bytes 25165824 | tf_op jit(solution)/shard_map/attend/pallas_call | solution.py:339
  26.8 2.6 %merge_pair.1 = f32[25,64,128]{2,1,0:T(8,128)S(1)} custom-call(f32[24,128,128]{2,1,0:T(8,128)S(1)} %get-tuple-element.23.numer, f32[128,128]{1,0:T(8,128)S(1)} %get-tuple-element.24.stats), custom_call_target="tpu_custom_call" | custom-call | tf_op jit(solution)/shard_map/merge_pair/pallas_call | solution.py:413
  29.4 2.0 %collective-permute-start = (f32[25,64,128]{2,1,0:T(8,128)S(1)}, f32[25,64,128]{2,1,0:T(8,128)S(1)}, u32[]{:S(2)}, u32[]{:S(2)}) collective-permute-start(f32[25,64,128]{2,1,0:T(8,128)S(1)} %merge_pair.1), channel_id=1, source_target_pairs={{0,2},{1,3},{2,0},{3,1},{4,6},{5,7},{6,4},{7,5},{8,10},{9,11},{10,... | collective-permute-start | bytes 2457608 | tf_op jit(solution)/shard_map/ppermute | solution.py:591
  31.4 18.7 %attend.3 = (bf16[64,1024,128]{2,1,0:T(8,128)(2,1)}, bf16[64,1024,128]{2,1,0:T(8,128)(2,1)}, f32[40,128,128]{2,1,0:T(8,128)S(1)}, f32[128,128]{1,0:T(8,128)S(1)}) custom-call(s32[64]{0:T(128)S(1)} %copy-done, bf16[64,1024,128]{2,1,0:T(8,128)(2,1)} %bitcast.22, bf16[64,1024,128]{2,1,0:T(8,128)(2,1)} %bitcast.24, ...), custom_call_target="tpu_custom_call", output_to_operand_aliasing={{0}: (6, {}), {1}: (7, {})} | custom-call | flops 2684354560 | bytes 41943040 | tf_op jit(solution)/shard_map/attend/pallas_call | solution.py:339
  50.1 0.0 collective-permute-done
  50.1 0.0 copy-start.1
  50.1 37.6 %merge.1 = (f32[4,64,4096]{2,1,0:T(8,128)S(1)}, f32[4,64,4096]{2,1,0:T(8,128)S(1)}) custom-call(f32[40,128,128]{2,1,0:T(8,128)S(1)} %get-tuple-element.21.numer, f32[128,128]{1,0:T(8,128)S(1)} %get-tuple-element.22.stats, f32[25,4,2,8,128]{4,3,2,1,0:T(8,128)S(1)} %bitcast.19, f32[25,4,2,8,128]{4,3,2,1,0:T(8,128)S(1)} %bitcast.20, bf16[4096,4096]{1,0:T(8,128)(2,1)} %wo_hbm.1), custom_call_target="tpu_custom_call" | custom-call | tf_op jit(solution)/shard_map/merge/pallas_call | solution.py:555
  87.7 0.0 copy-done.1
  87.7 2.3 %add_convert_fusion = bf16[4,64,4096]{2,1,0:T(8,128)(2,1)} fusion(f32[4,64,4096]{2,1,0:T(8,128)S(1)} %get-tuple-element.25, f32[4,64,4096]{2,1,0:T(8,128)S(1)} %get-tuple-element.26, bf16[4,64,4096]{2,1,0:T(8,128)(2,1)S(1)} %copy-done.1), kind=kLoop, calls=%fused_computation | loop fusion | flops 4194304 | bytes 12582912 | tf_op jit(solution)/shard_map/convert_element_type | solution.py:594
Async XLA Ops:
  0.6 13.6 %copy-start = (s32[64]{0:T(128)S(1)}, s32[64]{0:T(128)}, u32[]{:S(2)}) copy-start(s32[64]{0:T(128)} %refs_0_.1) | copy-start | bytes 772
  29.4 20.6 %collective-permute-start = (f32[25,64,128]{2,1,0:T(8,128)S(1)}, f32[25,64,128]{2,1,0:T(8,128)S(1)}, u32[]{:S(2)}, u32[]{:S(2)}) collective-permute-start(f32[25,64,128]{2,1,0:T(8,128)S(1)} %merge_pair.1), channel_id=1, source_target_pairs={{0,2},{1,3},{2,0},{3,1},{4,6},{5,7},{6,4},{7,5},{8,10},{9,11},{10,... | collective-permute-start | bytes 2457608 | tf_op jit(solution)/shard_map/ppermute | solution.py:591
  50.1 37.6 %copy-start.1 = (bf16[4,64,4096]{2,1,0:T(8,128)(2,1)S(1)}, bf16[4,64,4096]{2,1,0:T(8,128)(2,1)}, u32[]{:S(2)}) copy-start(bf16[4,64,4096]{2,1,0:T(8,128)(2,1)} %param.11) | copy-start | bytes 6291460

commit v9 on v8

--- a/solution.py
+++ b/solution.py
@@ -101,6 +101,7 @@
         if n == 0:
             w_copies[1].start()
         norm_piece(n * piece)
+    w_copies[2].start()
 
     def finish(n):
         w_hbm, out_ref, sems, total, i = blocks[n]
@@ -125,8 +126,8 @@
     sends = []
     for n in range(len(blocks)):
         w_copies[n].wait()
-        if n + 2 < len(blocks):
-            w_copies[n + 2].start()
+        if n + 3 < len(blocks):
+            w_copies[n + 3].start()
         acc[n % 2] = jnp.dot(normed[...], wbuf[n], preferred_element_type=F32)
         if n > 0:
             finish(n - 1)

time: 90 us -> 90.1 us (level)
  no operation moved by 1% of the time
where the time goes in v9:
time: 90.1 us; the launch traced here: 90.3 us
  Pallas kernels  85 us (94%)
  starting transfers between devices  2.28 us (3%)
  other arithmetic  2.28 us (3%)
    pallas_call x1, Pallas kernels, merge(): pl.pallas_call(functools.partial(merge_kernel, early_chunks, chunks, step...  37.6 us
    pallas_call x2, Pallas kernels, attend(): pl.pallas_call(continued if partial else kernel, name='attend', in_specs=...  31.2 us
    pallas_call x1, Pallas kernels, project(): pl.pallas_call(functools.partial(project_kernel, width, heads, kv_heads,...  13.5 us
    pallas_call x1, Pallas kernels, merge_pair(): pl.pallas_call(functools.partial(pair_kernel, chunks, batch), name='merge...  2.63 us
    convert_element_type x1, other arithmetic, per_device(): y_steps = (x_steps.astype(F32) + (own + other)).astype(BF16)  2.28 us
    ppermute x1, starting transfers between devices, per_device(): lax.ppermute(early_own, 'sp', [(i, (i + 2) % 4) for i in range(4)])  2.28 us
  transfers between devices with their start and end apart: 1, of which 0 were waited for; matrix products, arithmetic and copies ran while one was open for 0% of the time, Pallas kernels for 21%

profile of v9, /device:TPU:0, one launch (start us, length us, event | category | flops | bytes accessed | tf_op | source)
XLA Modules:
  0.0 90.3 jit_solution(756547190660505318)
XLA Ops:
  0.6 0.0 copy-start
  0.6 13.5 %project.1 = (f32[32,32,8,128]{3,2,1,0:T(8,128)S(1)}, f32[32,8,8,128]{3,2,1,0:T(8,128)S(1)}, f32[32,8,8,128]{3,2,1,0:T(8,128)S(1)}) custom-call(s32[64]{0:T(128)} %refs_0_.1, bf16[256,4096]{1,0:T(8,128)(2,1)} %bitcast.27, bf16[32,128]{1,0:T(8,128)(2,1)} %bitcast.28, bf16[1,128]{1,0:T(2,128)(2,1)} %bitcast.29, bf16[1,128]{1,0:T(2,128)(2,1)} %bitcast.30, ...), custom_call_target="tpu_custom_call" | custom-call | tf_op jit(solution)/shard_map/project/pallas_call | solution.py:150
  14.2 0.0 copy-done
  14.2 12.5 %attend.2 = (bf16[64,1024,128]{2,1,0:T(8,128)(2,1)}, bf16[64,1024,128]{2,1,0:T(8,128)(2,1)}, f32[24,128,128]{2,1,0:T(8,128)S(1)}, f32[128,128]{1,0:T(8,128)S(1)}) custom-call(s32[64]{0:T(128)S(1)} %copy-done, bf16[64,1024,128]{2,1,0:T(8,128)(2,1)} %bitcast.21, bf16[64,1024,128]{2,1,0:T(8,128)(2,1)} %bitcast.23, f32[8192,128]{1,0:T(8,128)S(1)} %bitcast.13, ...), custom_call_target="tpu_custom_call" | custom-call | flops 1610612736 | bytes 25165824 | tf_op jit(solution)/shard_map/attend/pallas_call | solution.py:340
  26.7 2.6 %merge_pair.1 = f32[25,64,128]{2,1,0:T(8,128)S(1)} custom-call(f32[24,128,128]{2,1,0:T(8,128)S(1)} %get-tuple-element.23.numer, f32[128,128]{1,0:T(8,128)S(1)} %get-tuple-element.24.stats), custom_call_target="tpu_custom_call" | custom-call | tf_op jit(solution)/shard_map/merge_pair/pallas_call | solution.py:414
  29.3 2.3 %collective-permute-start = (f32[25,64,128]{2,1,0:T(8,128)S(1)}, f32[25,64,128]{2,1,0:T(8,128)S(1)}, u32[]{:S(2)}, u32[]{:S(2)}) collective-permute-start(f32[25,64,128]{2,1,0:T(8,128)S(1)} %merge_pair.1), channel_id=1, source_target_pairs={{0,2},{1,3},{2,0},{3,1},{4,6},{5,7},{6,4},{7,5},{8,10},{9,11},{10,... | collective-permute-start | bytes 2457608 | tf_op jit(solution)/shard_map/ppermute | solution.py:592
  31.6 18.8 %attend.3 = (bf16[64,1024,128]{2,1,0:T(8,128)(2,1)}, bf16[64,1024,128]{2,1,0:T(8,128)(2,1)}, f32[40,128,128]{2,1,0:T(8,128)S(1)}, f32[128,128]{1,0:T(8,128)S(1)}) custom-call(s32[64]{0:T(128)S(1)} %copy-done, bf16[64,1024,128]{2,1,0:T(8,128)(2,1)} %bitcast.22, bf16[64,1024,128]{2,1,0:T(8,128)(2,1)} %bitcast.24, ...), custom_call_target="tpu_custom_call", output_to_operand_aliasing={{0}: (6, {}), {1}: (7, {})} | custom-call | flops 2684354560 | bytes 41943040 | tf_op jit(solution)/shard_map/attend/pallas_call | solution.py:340
  50.4 0.0 collective-permute-done
  50.4 0.0 copy-start.1
  50.4 37.6 %merge.1 = (f32[4,64,4096]{2,1,0:T(8,128)S(1)}, f32[4,64,4096]{2,1,0:T(8,128)S(1)}) custom-call(f32[40,128,128]{2,1,0:T(8,128)S(1)} %get-tuple-element.21.numer, f32[128,128]{1,0:T(8,128)S(1)} %get-tuple-element.22.stats, f32[25,4,2,8,128]{4,3,2,1,0:T(8,128)S(1)} %bitcast.19, f32[25,4,2,8,128]{4,3,2,1,0:T(8,128)S(1)} %bitcast.20, bf16[4096,4096]{1,0:T(8,128)(2,1)} %wo_hbm.1), custom_call_target="tpu_custom_call" | custom-call | tf_op jit(solution)/shard_map/merge/pallas_call | solution.py:556
  88.0 0.0 copy-done.1
  88.0 2.3 %add_convert_fusion = bf16[4,64,4096]{2,1,0:T(8,128)(2,1)} fusion(f32[4,64,4096]{2,1,0:T(8,128)S(1)} %get-tuple-element.25, f32[4,64,4096]{2,1,0:T(8,128)S(1)} %get-tuple-element.26, bf16[4,64,4096]{2,1,0:T(8,128)(2,1)S(1)} %copy-done.1), kind=kLoop, calls=%fused_computation | loop fusion | flops 4194304 | bytes 12582912 | tf_op jit(solution)/shard_map/convert_element_type | solution.py:595
Async XLA Ops:
  0.6 13.6 %copy-start = (s32[64]{0:T(128)S(1)}, s32[64]{0:T(128)}, u32[]{:S(2)}) copy-start(s32[64]{0:T(128)} %refs_0_.1) | copy-start | bytes 772
  29.3 21.1 %collective-permute-start = (f32[25,64,128]{2,1,0:T(8,128)S(1)}, f32[25,64,128]{2,1,0:T(8,128)S(1)}, u32[]{:S(2)}, u32[]{:S(2)}) collective-permute-start(f32[25,64,128]{2,1,0:T(8,128)S(1)} %merge_pair.1), channel_id=1, source_target_pairs={{0,2},{1,3},{2,0},{3,1},{4,6},{5,7},{6,4},{7,5},{8,10},{9,11},{10,... | collective-permute-start | bytes 2457608 | tf_op jit(solution)/shard_map/ppermute | solution.py:592
  50.4 37.6 %copy-start.1 = (bf16[4,64,4096]{2,1,0:T(8,128)(2,1)S(1)}, bf16[4,64,4096]{2,1,0:T(8,128)(2,1)}, u32[]{:S(2)}) copy-start(bf16[4,64,4096]{2,1,0:T(8,128)(2,1)} %param.11) | copy-start | bytes 6291460
